TPU v7x, 256 devices: a 8x8x2 block of a 8x8x16 slice. The times are simulated.
256 devices in a mesh: cosmo: 2 (over z), row: 128 (over y, x, core).
Axes of the slice: x: 8, y: 8, z: 2, core: 2. Of those that a mesh axis runs over, the one named last changes fastest.
The devices are a block of a 8x8x16 slice.
Arguments:
- potentials: float32 [4, 2048, 16384], P('cosmo', 'row'), parts along dimension 0, may hold values from -3 to 3
- ratios: float32 [6], P('cosmo'), parts along dimension 0, may hold values from 0.3 to 0.9
- row_offset: int32 [256], P('cosmo'), parts along dimension 0, may hold values from 0 to 7
- col_offset: int32 [256], P('cosmo'), parts along dimension 0, may hold values from 0 to 127
Outputs:
- convergence: float32 [4096, 16384], P(('cosmo', 'row')), parts along dimension 0
- shear_map: float32 [2, 4096, 16384], P(None, ('cosmo', 'row')), parts along dimension 1
- rotation: float32 [4096, 16384], P(('cosmo', 'row')), parts along dimension 0
- displacement: float32 [2, 4096, 16384], P(None, ('cosmo', 'row')), parts along dimension 1
There are 2 independent parts, one for each index of `cosmo`. A program takes and returns all parts, laid end to end along the dimension named above; each array names one. Nothing has to cross between parts.
Inputs may be any that keep to these rules, and one draw needn't show every extreme that they name: `row_offset`: row offsets count blocks of 256 rows.
All inputs are finite; a program needn't handle non-finite values.
Results may differ from a plain program's by a relative error of at most 0.00002.
Values sent between devices are 32-bit elements; how exact they have to be, the bound alone decides.
A program may use at most 128 MiB of HBM per device.

v0:
```python
import jax
import jax.numpy as jnp
from jax import lax
from jax.sharding import PartitionSpec as P

BITS = 3
RB = 8


def with_halo(cells, sides, width):
    for axis, dim in sides:
        count = lax.axis_size(axis)
        head = lax.slice_in_dim(cells, 0, width, axis=dim)
        tail = lax.slice_in_dim(cells, cells.shape[dim] - width, cells.shape[dim], axis=dim)
        cells = jnp.concatenate(
            [
                lax.ppermute(tail, axis, [(i, (i + 1) % count) for i in range(count)]),
                cells,
                lax.ppermute(head, axis, [((i + 1) % count, i) for i in range(count)]),
            ],
            axis=dim,
        )
    return cells


def passed_along(x, axis, by):
    size = lax.axis_size(axis)
    return lax.ppermute(x, axis, [(i, (i + by) % size) for i in range(size)])


def column_slope(field):
    return (
        8.0 * (jnp.roll(field, -1, 2) - jnp.roll(field, 1, 2))
        - (jnp.roll(field, -2, 2) - jnp.roll(field, 2, 2))
    ) / 12.0


def row_slope(padded, height):
    return (
        8.0 * (padded[:, 3 : height + 3] - padded[:, 1 : height + 1])
        - (padded[:, 4 : height + 4] - padded[:, 0:height])
    ) / 12.0


def derive(field):
    height = field.shape[1]
    padded = with_halo(field, (("row", 1),), 4)
    widened = row_slope(padded, height + 4)
    slope_r = widened[:, 2 : height + 2]
    curve_rr = row_slope(widened, height)
    slope_c = column_slope(field)
    return (slope_r, slope_c, curve_rr, column_slope(slope_r), column_slope(slope_c))


def assemble(nearer, farther, ratios):
    near_r, near_c, near_rr, near_rc, near_cc = nearer
    far_r, far_c, far_rr, far_rc, far_cc = farther
    beta_near = ratios[0]
    beta_one = ratios[1]
    beta_two = ratios[2]
    inner_rr = 1.0 - beta_near * near_rr
    inner_rc = -beta_near * near_rc
    inner_cc = 1.0 - beta_near * near_cc
    chain_rr = far_rr * inner_rr + far_rc * inner_rc
    chain_rc = far_rr * inner_rc + far_rc * inner_cc
    chain_cr = far_rc * inner_rr + far_cc * inner_rc
    chain_cc = far_rc * inner_rc + far_cc * inner_cc
    total_rr = 1.0 - beta_one * near_rr - beta_two * chain_rr
    total_rc = -beta_one * near_rc - beta_two * chain_rc
    total_cr = -beta_one * near_rc - beta_two * chain_cr
    total_cc = 1.0 - beta_one * near_cc - beta_two * chain_cc
    convergence = 1.0 - 0.5 * (total_rr + total_cc)
    shear_map = jnp.stack([0.5 * (total_rr - total_cc), -0.5 * (total_rc + total_cr)])
    rotation = 0.5 * (total_rc - total_cr)
    displacement = jnp.stack(
        [beta_one * near_r + beta_two * far_r, beta_one * near_c + beta_two * far_c]
    )
    return (convergence, shear_map, rotation, displacement)


def per_device(potentials, ratios, row_offset, col_offset):
    devices = lax.axis_size("row")
    height = potentials.shape[1]
    columns = potentials.shape[2]
    blocks = columns // 128
    source = (jnp.arange(blocks, dtype=jnp.int32) + col_offset) % blocks
    stride = devices // RB
    fields = derive(potentials[0:1])
    nearer = tuple((member[0] for member in fields))
    strips = potentials[1].reshape(height, blocks, 128)
    left_part = jnp.take(strips, (source - 1) % blocks, axis=1)[:, :, 64:]
    middle_part = jnp.take(strips, source, axis=1)
    right_part = jnp.take(strips, (source + 1) % blocks, axis=1)[:, :, :64]
    windows = jnp.concatenate([left_part, middle_part, right_part], axis=2)
    for bit_level in range(BITS):
        arrived = passed_along(windows, "row", devices - stride * 2**bit_level)
        picked = (row_offset // 2**bit_level % 2 == 1).reshape(1, blocks, 1)
        windows = jnp.where(picked, arrived, windows)
    derived = derive(windows.reshape(1, height, blocks * 256))
    farther = tuple(
        (
            member[0].reshape(height, blocks, 256)[:, :, 64:192].reshape(height, columns)
            for member in derived
        )
    )
    return assemble(nearer, farther, ratios)


def solution(mesh):
    return jax.shard_map(
        per_device,
        mesh=mesh,
        in_specs=(P("cosmo", "row", None), P("cosmo"), P("cosmo"), P("cosmo")),
        out_specs=(
            P(("cosmo", "row"), None),
            P(None, ("cosmo", "row"), None),
            P(("cosmo", "row"), None),
            P(None, ("cosmo", "row"), None),
        ),
        check_vma=False,
    )
```

profile of v0, /device:TPU:543, one launch (start us, length us, event | category | flops | bytes accessed | tf_op | source)
XLA Modules:
  0.0 413.0 jit_solution(15362464744143215431)
XLA Ops:
  1.4 1.7 fusion.72
  4.6 1.7 gather_fusion.1
  6.4 1.7 gather_fusion
  8.1 1.5 select_bitcast_fusion.2
  10.9 2.2 pad_maximum_fusion.1
  14.1 1.8 collective-permute-start
  15.9 1.7 fusion.67
  17.6 1.7 fusion.69
  22.4 1.8 collective-permute-done.1
  24.2 1.2 pad_maximum_fusion.4
  25.4 1.7 fusion.17
  27.3 36.8 %collective-permute-done.2 = f32[16,128,256]{2,0,1:T(8,128)} collective-permute-done((f32[16,128,256]{2,0,1:T(8,128)}, f32[16,128,256]{2,0,1:T(8,128)}, u32[]{:S(2)}, u32[]{:S(2)}) %collective-permute-start.2) | collective-permute-done | bytes 2097184 | tf_op jit(solution)/shard_map/ppermute | solution.py:28
  64.2 2.6 broadcast_select_fusion
  66.8 10.3 %collective-permute-start.3 = (f32[16,128,256]{2,0,1:T(8,128)S(1)}, f32[16,128,256]{2,0,1:T(8,128)S(1)}, u32[]{:S(2)}, u32[]{:S(2)}) collective-permute-start(f32[16,128,256]{2,0,1:T(8,128)S(1)} %broadcast_select_fusion), channel_id=1, source_target_pairs={{0,96},{1,97},{2,98},{3,99},{4,100},{5,101},{6,102},{7,103},{8,104... | collective-permute-start | bytes 6291464 | tf_op jit(solution)/shard_map/ppermute | solution.py:28
  77.1 2.4 fusion.82
  79.4 86.7 %collective-permute-done.3 = f32[16,128,256]{2,0,1:T(8,128)S(1)} collective-permute-done((f32[16,128,256]{2,0,1:T(8,128)S(1)}, f32[16,128,256]{2,0,1:T(8,128)S(1)}, u32[]{:S(2)}, u32[]{:S(2)}) %collective-permute-start.3) | collective-permute-done | bytes 2097184 | tf_op jit(solution)/shard_map/ppermute | solution.py:28
  166.4 3.5 collective-permute-start.4
  170.0 2.5 fusion.84
  172.5 74.7 %collective-permute-done.4 = f32[16,128,256]{2,0,1:T(8,128)S(1)} collective-permute-done((f32[16,128,256]{2,0,1:T(8,128)S(1)}, f32[16,128,256]{2,0,1:T(8,128)S(1)}, u32[]{:S(2)}, u32[]{:S(2)}) %collective-permute-start.4) | collective-permute-done | bytes 2097184 | tf_op jit(solution)/shard_map/ppermute | solution.py:28
  247.4 2.5 copy.35
  250.0 1.7 reshape.1215
  254.4 1.2 fusion.11
  257.8 1.2 mul.479
  259.0 4.1 multiply_add_fusion
  263.2 2.4 fusion.86
  265.6 2.5 fusion.88
  269.6 81.0 %collective-permute-start.5 = (f32[1,4,32768]{2,1,0:T(4,128)}, f32[1,4,32768]{2,1,0:T(4,128)}, u32[]{:S(2)}, u32[]{:S(2)}) collective-permute-start(f32[1,4,32768]{2,1,0:T(4,128)} %get-tuple-element.41), channel_id=1, source_target_pairs={{0,1},{1,2},{2,3},{3,4},{4,5},{5,6},{6,7},{7,8},{8,9},{9,10},{10,1... | collective-permute-start | bytes 1572872 | tf_op jit(solution)/shard_map/ppermute | solution.py:17
  352.4 1.3 slice.426
  353.7 2.4 reshape.1221
  357.1 4.6 %collective-permute-done.6 = f32[1,4,32768]{2,1,0:T(4,128)} collective-permute-done((f32[1,4,32768]{2,1,0:T(4,128)}, f32[1,4,32768]{2,1,0:T(4,128)}, u32[]{:S(2)}, u32[]{:S(2)}) %collective-permute-start.6) | collective-permute-done | bytes 524320 | tf_op jit(solution)/shard_map/ppermute | solution.py:19
  361.6 1.6 pad_maximum_fusion
  363.3 2.5 fusion.2
  365.8 2.2 fusion.62
  368.0 2.7 fusion.64
  370.7 2.7 fusion.66
  375.3 1.2 mul.476
  376.4 3.1 fusion.35
  379.5 4.0 fusion.8
  384.5 1.2 copy-done.16
  386.4 1.3 slice.384
  387.7 1.2 reshape.1220
  388.9 2.4 reshape.1219
  391.3 3.1 pad_maximum_fusion.3
  394.6 8.4 %fusion.28 = (f32[16,16384]{1,0:T(8,128)}, f32[1,16,16384]{2,1,0:T(8,128)S(1)}, f32[16,16384]{1,0:T(8,128)S(1)}, f32[16,16384]{1,0:T(8,128)S(1)}) fusion(f32[2,8,128,128]{3,2,1,0:T(8,128)S(1)} %bitcast.125, f32[2,8,128,128]{3,2,1,0:T(8,128)S(1)} %bitcast.127, f32[2,8,128,128]{3,2,1,0:T(8,128)S(1)} %bitcast.129, f32[]{:T(128)S(6)} %mul.452, f32[]{:T(128)} %bitcast.6, ...), kind=kLoop, calls=%fused_computation.50 | loop fusion | flops 9961472 | bytes 19925636 | tf_op jit(solution)/shard_map/mul | solution.py:74
  403.1 2.8 subtract_multiply_fusion
  406.0 1.2 add_multiply_fusion
  407.2 1.5 pad_maximum_fusion.2
  408.7 3.9 fusion.23
  (109 shorter events, 18.7 us)
Async XLA Ops:
  8.1 1.9 copy-start.18
  10.0 1.0 copy-start.14
  10.3 2.8 copy-start.10
  10.3 2.8 copy-start.12
  10.9 2.2 copy-start.4
  13.1 51.0 %collective-permute-start.2 = (f32[16,128,256]{2,0,1:T(8,128)}, f32[16,128,256]{2,0,1:T(8,128)}, u32[]{:S(2)}, u32[]{:S(2)}) collective-permute-start(f32[16,128,256]{2,0,1:T(8,128)} %pad_maximum_fusion.1), channel_id=1, source_target_pairs={{0,112},{1,113},{2,114},{3,115},{4,116},{5,117},{6,118},{7,119},{8... | collective-permute-start | bytes 6291464 | tf_op jit(solution)/shard_map/ppermute | solution.py:28
  14.1 8.4 %collective-permute-start = (f32[1,4,16384]{2,1,0:T(4,128)}, f32[1,4,16384]{2,1,0:T(4,128)S(1)}, u32[]{:S(2)}, u32[]{:S(2)}) collective-permute-start(f32[1,4,16384]{2,1,0:T(4,128)} %get-tuple-element.37), channel_id=1, source_target_pairs={{0,1},{1,2},{2,3},{3,4},{4,5},{5,6},{6,7},{7,8},{8,9},{9,10},{10,1... | collective-permute-start | bytes 786440 | tf_op jit(solution)/shard_map/ppermute | solution.py:17
  15.9 8.3 %collective-permute-start.1 = (f32[1,4,16384]{2,1,0:T(4,128)}, f32[1,4,16384]{2,1,0:T(4,128)}, u32[]{:S(2)}, u32[]{:S(2)}) collective-permute-start(f32[1,4,16384]{2,1,0:T(4,128)} %get-tuple-element.38), channel_id=1, source_target_pairs={{1,0},{2,1},{3,2},{4,3},{5,4},{6,5},{7,6},{8,7},{9,8},{10,9},{11,1... | collective-permute-start | bytes 786440 | tf_op jit(solution)/shard_map/ppermute | solution.py:19
  17.6 1.7 copy-start.30
  17.6 1.8 copy-start.29
  25.4 38.8 %copy-start.11 = (f32[16,128,128]{2,0,1:T(8,128)S(1)}, f32[16,128,128]{2,0,1:T(8,128)}, u32[]{:S(2)}) copy-start(f32[16,128,128]{2,0,1:T(8,128)} %copy-done.10) | copy-start | bytes 3145732
  25.4 38.8 %copy-start.13 = (f32[16,128,128]{2,0,1:T(8,128)S(1)}, f32[16,128,128]{2,0,1:T(8,128)}, u32[]{:S(2)}) copy-start(f32[16,128,128]{2,0,1:T(8,128)} %copy-done.12) | copy-start | bytes 3145732
  25.4 38.8 %copy-start.15 = (f32[16,128,64]{2,0,1:T(8,128)S(1)}, f32[16,128,64]{2,0,1:T(8,128)}, u32[]{:S(2)}) copy-start(f32[16,128,64]{2,0,1:T(8,128)} %copy-done.14) | copy-start | bytes 1572868
  27.2 142.8 %copy-start = (f32[1,20,16384]{2,1,0:T(8,128)}, f32[1,20,16384]{2,1,0:T(8,128)S(1)}, u32[]{:S(2)}) copy-start(f32[1,20,16384]{2,1,0:T(8,128)S(1)} %fusion.17) | copy-start | bytes 3932164
  66.8 99.4 %collective-permute-start.3 = (f32[16,128,256]{2,0,1:T(8,128)S(1)}, f32[16,128,256]{2,0,1:T(8,128)S(1)}, u32[]{:S(2)}, u32[]{:S(2)}) collective-permute-start(f32[16,128,256]{2,0,1:T(8,128)S(1)} %broadcast_select_fusion), channel_id=1, source_target_pairs={{0,96},{1,97},{2,98},{3,99},{4,100},{5,101},{6,102},{7,103},{8,104... | collective-permute-start | bytes 6291464 | tf_op jit(solution)/shard_map/ppermute | solution.py:28
  166.4 80.7 %collective-permute-start.4 = (f32[16,128,256]{2,0,1:T(8,128)S(1)}, f32[16,128,256]{2,0,1:T(8,128)S(1)}, u32[]{:S(2)}, u32[]{:S(2)}) collective-permute-start(f32[16,128,256]{2,0,1:T(8,128)S(1)} %broadcast_select_fusion.1), channel_id=1, source_target_pairs={{0,64},{1,65},{2,66},{3,67},{4,68},{5,69},{6,70},{7,71},{8,72},{9,... | collective-permute-start | bytes 6291464 | tf_op jit(solution)/shard_map/ppermute | solution.py:28
  255.5 1.3 copy-start.2
  265.6 2.5 copy-start.3
  269.6 87.4 %collective-permute-start.5 = (f32[1,4,32768]{2,1,0:T(4,128)}, f32[1,4,32768]{2,1,0:T(4,128)}, u32[]{:S(2)}, u32[]{:S(2)}) collective-permute-start(f32[1,4,32768]{2,1,0:T(4,128)} %get-tuple-element.41), channel_id=1, source_target_pairs={{0,1},{1,2},{2,3},{3,4},{4,5},{5,6},{6,7},{7,8},{8,9},{9,10},{10,1... | collective-permute-start | bytes 1572872 | tf_op jit(solution)/shard_map/ppermute | solution.py:17
  350.6 11.0 %collective-permute-start.6 = (f32[1,4,32768]{2,1,0:T(4,128)}, f32[1,4,32768]{2,1,0:T(4,128)}, u32[]{:S(2)}, u32[]{:S(2)}) collective-permute-start(f32[1,4,32768]{2,1,0:T(4,128)} %get-tuple-element.42), channel_id=1, source_target_pairs={{1,0},{2,1},{3,2},{4,3},{5,4},{6,5},{7,6},{8,7},{9,8},{10,9},{11,1... | collective-permute-start | bytes 1572872 | tf_op jit(solution)/shard_map/ppermute | solution.py:19
  374.2 2.3 copy-start.1
  376.4 3.1 copy-start.17
  384.2 1.6 copy-start.16
  391.3 3.2 copy-start.5
  391.3 3.2 copy-start.6
  391.3 3.2 copy-start.23
  391.3 3.2 copy-start.24
  394.5 8.5 %copy-start.7 = (f32[1,16,16384]{2,1,0:T(8,128)S(1)}, f32[1,16,16384]{2,1,0:T(8,128)}, u32[]{:S(2)}) copy-start(f32[1,16,16384]{2,1,0:T(8,128)} %reshape.1221) | copy-start | bytes 3145732
  394.5 8.5 %copy-start.8 = (f32[1,16,16384]{2,1,0:T(8,128)S(1)}, f32[1,16,16384]{2,1,0:T(8,128)}, u32[]{:S(2)}) copy-start(f32[1,16,16384]{2,1,0:T(8,128)} %reshape.1220) | copy-start | bytes 3145732
  394.5 8.5 %copy-start.9 = (f32[1,16,16384]{2,1,0:T(8,128)S(1)}, f32[1,16,16384]{2,1,0:T(8,128)}, u32[]{:S(2)}) copy-start(f32[1,16,16384]{2,1,0:T(8,128)} %reshape.1219) | copy-start | bytes 3145732
  394.5 8.5 %copy-start.19 = (f32[1,16,16383]{2,1,0:T(8,128)S(1)}, f32[1,16,16383]{2,1,0:T(8,128)}, u32[]{:S(2)}) copy-start(f32[1,16,16383]{2,1,0:T(8,128)} %get-tuple-element.59) | copy-start | bytes 3145540
  394.5 8.5 %copy-start.20 = (f32[1,16,16383]{2,1,0:T(8,128)S(1)}, f32[1,16,16383]{2,1,0:T(8,128)}, u32[]{:S(2)}) copy-start(f32[1,16,16383]{2,1,0:T(8,128)} %get-tuple-element.62) | copy-start | bytes 3145540
  394.5 8.5 %copy-start.21 = (f32[1,16,16382]{2,1,0:T(8,128)S(1)}, f32[1,16,16382]{2,1,0:T(8,128)}, u32[]{:S(2)}) copy-start(f32[1,16,16382]{2,1,0:T(8,128)} %get-tuple-element.67) | copy-start | bytes 3145348
  394.6 8.5 %copy-start.22 = (f32[1,16,16382]{2,1,0:T(8,128)S(1)}, f32[1,16,16382]{2,1,0:T(8,128)}, u32[]{:S(2)}) copy-start(f32[1,16,16382]{2,1,0:T(8,128)} %get-tuple-element.70) | copy-start | bytes 3145348
  394.6 8.5 %copy-start.25 = (f32[1,16,16383]{2,1,0:T(8,128)S(1)}, f32[1,16,16383]{2,1,0:T(8,128)}, u32[]{:S(2)}) copy-start(f32[1,16,16383]{2,1,0:T(8,128)} %get-tuple-element.75) | copy-start | bytes 3145540
  394.6 8.5 %copy-start.26 = (f32[1,16,16383]{2,1,0:T(8,128)S(1)}, f32[1,16,16383]{2,1,0:T(8,128)}, u32[]{:S(2)}) copy-start(f32[1,16,16383]{2,1,0:T(8,128)} %get-tuple-element.78) | copy-start | bytes 3145540
  394.6 8.5 %copy-start.27 = (f32[1,16,16382]{2,1,0:T(8,128)S(1)}, f32[1,16,16382]{2,1,0:T(8,128)}, u32[]{:S(2)}) copy-start(f32[1,16,16382]{2,1,0:T(8,128)} %get-tuple-element.83) | copy-start | bytes 3145348
  394.6 8.5 %copy-start.28 = (f32[1,16,16382]{2,1,0:T(8,128)S(1)}, f32[1,16,16382]{2,1,0:T(8,128)}, u32[]{:S(2)}) copy-start(f32[1,16,16382]{2,1,0:T(8,128)} %get-tuple-element.86) | copy-start | bytes 3145348
where the time goes:
time: 421 us; the launch traced here: 413 us
  waiting for transfers between devices  205 us (49%)
  starting transfers between devices  96.7 us (23%)
  other arithmetic  53.8 us (13%)
  local copies, waits for them, and re-layouts  53.1 us (13%)
    ppermute x3, waiting for transfers between devices, passed_along(): return lax.ppermute(x, axis, [(i, (i + by) % size) for i in range(size)])  198 us
    ppermute x2, starting transfers between devices, with_halo(): lax.ppermute(tail, axis, [(i, (i + 1) % count) for i in range(count)])  82.8 us
    ppermute x3, starting transfers between devices, passed_along(): return lax.ppermute(x, axis, [(i, (i + by) % size) for i in range(size)])  13.8 us
  transfers between devices with their start and end apart: 7, of which 6 were waited for; matrix products, arithmetic and copies ran while one was open for 4% of the time, Pallas kernels for 0%

commit v1 on v0

v1 whole, which is shorter than its diff:
```python
import functools

import jax
import jax.numpy as jnp
from jax import lax
from jax.experimental import pallas as pl
from jax.experimental.pallas import tpu as pltpu
from jax.sharding import PartitionSpec as P

RB = 8
LANES = 128
HALF = RB // 2
GROUP = 16
MESH = pl.DeviceIdType.MESH

PLANS = ((4, 3, 2, 1), (8, 8, 8, 4))


def chunk_base(plan):
    base, total = [], 0
    for count in plan:
        base.append(total)
        total += count
    return base, total


def iota(shape, dim):
    return lax.broadcasted_iota(jnp.int32, shape, dim)


def table_kernel(row_ref, col_ref, tab_ref):
    blocks = row_ref.shape[1]
    f32 = jnp.float32
    row = row_ref[...].astype(f32)
    lane = iota((1, blocks), 1)
    lane_f = lane.astype(f32)
    source = lane_f + col_ref[...].astype(f32)
    source = jnp.where(source >= blocks, source - blocks, source)
    sub2 = iota((blocks, blocks), 0)
    lane2 = iota((blocks, blocks), 1)

    def column(v):
        return jnp.sum(jnp.where(sub2 == lane2, jnp.broadcast_to(v, (blocks, blocks)), 0.0), axis=1, keepdims=True)

    def total(v):
        return jnp.sum(v, axis=1, keepdims=True)

    halfway = (row == HALF).astype(f32)
    dist = jnp.where(row <= HALF, row, RB - row)
    n_half = total(halfway)
    load_a = total(jnp.where(row < HALF, row, 0.0))
    load_b = total(jnp.where(row > HALF, RB - row, 0.0))
    take_a = jnp.clip(jnp.floor((load_b + HALF * n_half - load_a) / (2 * HALF) + 0.5), 0.0, n_half)
    rank_half = jnp.sum(jnp.where(sub2 < lane2, jnp.broadcast_to(column(halfway), (blocks, blocks)), 0.0), axis=0, keepdims=True)
    way = jnp.where(row == 0, 0.0, jnp.where(row < HALF, 1.0, 2.0))
    way = jnp.where((row == HALF) & (rank_half < take_a), 1.0, way)
    big = 4096.0
    key = way * big + (HALF - dist) * blocks + lane_f
    key_c = jnp.broadcast_to(column(key), (blocks, blocks))
    key_r = jnp.broadcast_to(key, (blocks, blocks))
    way_r = jnp.broadcast_to(way, (blocks, blocks))
    ahead = (key_c < key_r) & (key_c >= way_r * big)
    slot = jnp.sum(ahead.astype(f32), axis=0, keepdims=True)
    slot_c = jnp.broadcast_to(column(slot), (blocks, blocks))
    way_c = jnp.broadcast_to(column(way), (blocks, blocks))
    source_c = jnp.broadcast_to(column(source), (blocks, blocks))
    here = slot_c == lane2.astype(f32)
    send = [
        jnp.sum(jnp.where(here & (way_c == w), source_c, 0.0), axis=0, keepdims=True) for w in (1.0, 2.0)
    ]
    fits = jnp.ones((1, 1), f32)
    for hop, count in enumerate(PLANS[0]):
        for w in (1.0, 2.0):
            need = total(((way == w) & (dist > hop)).astype(f32))
            fits = jnp.where(need > count * GROUP, 0.0, fits)
    chunk = jnp.floor(slot / GROUP)
    within = slot - chunk * GROUP
    spot = []
    for plan in PLANS:
        base, number = chunk_base(plan)
        at = jnp.zeros((1, blocks), f32)
        for hop in range(HALF):
            at = jnp.where(dist == hop + 1, float(base[hop]), at)
        spot.append(at + chunk + jnp.where(way == 2.0, float(number), 0.0))
    spot = jnp.where(fits > 0, spot[0], spot[1])
    spot = jnp.where(way == 0, 0.0, spot)
    within = jnp.where(way == 0, 0.0, within)
    turn = 8.0 * (lane_f - GROUP * jnp.floor(lane_f / GROUP) - within)
    turn = jnp.where(turn < 0, turn + LANES, turn)
    rows = [
        send[0],
        send[1],
        spot * (GROUP + 1) + within,
        spot * (GROUP + 1) + GROUP,
        turn,
        source,
        (way == 0).astype(f32),
        jnp.broadcast_to(1.0 - fits, (1, blocks)),
    ]
    tab_ref[...] = jnp.concatenate(rows, axis=0).astype(jnp.int32)


def exchange_kernel(plan, tab, pot, w_ref, h_ref, h1_ref, p1, p2, tiles, sent, got, en, ep, gn, gp, en1, ep1, gn1, gp1,
                    local_sem, send_sem, recv_sem, edge_send, edge_recv):
    base, number = chunk_base(plan)
    size = lax.axis_size("row")
    stride = size // RB
    me = lax.axis_index("row")
    blocks = p2.shape[1] // LANES
    rows = p2.shape[0]
    top = rows - 8
    packet = GROUP + 1
    first = plan[0]

    load2 = pltpu.make_async_copy(pot.at[1], p2, local_sem.at[0])
    load1 = pltpu.make_async_copy(pot.at[0], p1, local_sem.at[1])
    load2.start()
    load1.start()
    barrier = pltpu.get_barrier_semaphore()
    for by in (stride, size - stride, 1, size - 1):
        pl.semaphore_signal(barrier, inc=1, device_id={"row": lax.rem(me + by, size)}, device_id_type=MESH)

    lane = iota((rows, LANES), 1)
    lane_group = lane // 8
    sub = iota((8, LANES), 0)

    def tile(ref, s):
        return ref[s]

    def split(i, carry):
        for j in range(GROUP):
            tiles[i * GROUP + j] = p2[:, pl.ds(pl.multiple_of((i * GROUP + j) * LANES, LANES), LANES)]
        return carry

    def sides(ref, s):
        before = tile(ref, lax.rem(s + (blocks - 1), blocks))
        after = tile(ref, lax.rem(s + 1, blocks))
        return jnp.where(lane >= LANES // 2, before, after)

    def pack(i):
        way = lax.rem(i, 2)
        chunk = i // 2
        halo = jnp.zeros((rows, LANES), jnp.float32)
        for j in range(GROUP):
            s = tab[way, chunk * GROUP + j]
            sent[i * packet + j] = tile(tiles, s)
            halo = jnp.where(lane_group == j, pltpu.roll(sides(tiles, s), (8 * j + 4) % LANES, 1), halo)
        sent[i * packet + GROUP] = halo

    def toward(way):
        return {"row": lax.rem(me + jnp.where(way == 0, size - stride, stride), size)}

    def first_copy(i):
        way = lax.rem(i, 2)
        to = way * number + i // 2
        return pltpu.make_async_remote_copy(
            src_ref=sent.at[pl.ds(i * packet, packet)],
            dst_ref=got.at[pl.ds(to * packet, packet)],
            send_sem=send_sem.at[to],
            recv_sem=recv_sem.at[to],
            device_id=toward(way),
            device_id_type=MESH,
        )

    def relay(way, hop, c):
        origin = way * number + base[hop - 1] + c
        to = way * number + base[hop] + c
        return pltpu.make_async_remote_copy(
            src_ref=got.at[pl.ds(origin * packet, packet)],
            dst_ref=got.at[pl.ds(to * packet, packet)],
            send_sem=send_sem.at[to],
            recv_sem=recv_sem.at[to],
            device_id={"row": lax.rem(me + (size - stride if way == 0 else stride), size)},
            device_id_type=MESH,
        )

    def arrival(to):
        piece = got.at[pl.ds(to * packet, packet)]
        return pltpu.make_async_remote_copy(
            src_ref=piece, dst_ref=piece, send_sem=send_sem.at[to], recv_sem=recv_sem.at[to],
            device_id={"row": lax.rem(me + stride, size)}, device_id_type=MESH,
        )

    def edge(src, dst, by, at):
        return pltpu.make_async_remote_copy(
            src_ref=src, dst_ref=dst, send_sem=edge_send.at[at], recv_sem=edge_recv.at[at],
            device_id={"row": lax.rem(me + by, size)}, device_id_type=MESH,
        )

    load2.wait()
    lax.fori_loop(0, blocks // GROUP, split, 0)
    pack(0)
    pl.semaphore_wait(barrier, 4)

    def step(i, carry):
        pack(i)
        first_copy(i - 1).start()
        return carry

    lax.fori_loop(1, 2 * first, step, 0)
    first_copy(2 * first - 1).start()

    load1.wait()
    half = p1.shape[1] // 2
    width = 1024
    sub_w = iota((8, width), 0)

    def edges1(i, carry):
        at = pl.multiple_of(i * width, width)
        here, there = pl.ds(at, width), pl.ds(pl.multiple_of(at + half, width), width)
        en1[:, here] = jnp.where(sub_w >= 4, p1[top:, here], pltpu.roll(p1[top:, there], 4, 0))
        ep1[:, here] = jnp.where(sub_w < 4, p1[:8, here], pltpu.roll(p1[:8, there], 4, 0))
        return carry

    lax.fori_loop(0, half // width, edges1, 0)
    edge_down1 = edge(en1, gn1, 1, 0)
    edge_up1 = edge(ep1, gp1, size - 1, 1)

    for hop in range(1, HALF):
        for c in range(plan[hop]):
            for way in range(2):
                arrival(way * number + base[hop - 1] + c).wait_recv()
                relay(way, hop, c).start()
        if hop == 1:
            edge_down1.start()
            edge_up1.start()

    edge_down1.wait_recv()
    edge_up1.wait_recv()

    def halo1(i, carry):
        at = pl.multiple_of(i * width, width)
        here, there = pl.ds(at, width), pl.ds(pl.multiple_of(at + half, width), width)
        down, up = gn1[:, here], gp1[:, here]
        h1_ref[:, here] = jnp.where(sub_w >= 4, down, up)
        h1_ref[:, there] = pltpu.roll(jnp.where(sub_w < 4, down, up), 4, 0)
        return carry

    lax.fori_loop(0, half // width, halo1, 0)

    for hop in range(HALF):
        for c in range(plan[hop + 1] if hop + 1 < HALF else 0, plan[hop]):
            for way in range(2):
                arrival(way * number + base[hop] + c).wait_recv()

    quarter = blocks // GROUP // 2

    def fetch(b, j, halo):
        own = jnp.full((rows, LANES), tab[6, b], jnp.int32) > 0
        s = tab[5, b]
        value = jnp.where(own, tile(tiles, s), got[tab[2, b]])
        mine = pltpu.roll(sides(tiles, s), (8 * j + 4) % LANES, 1)
        theirs = got[tab[3, b]]
        turn = jnp.full((rows, LANES), tab[4, b], jnp.int32)
        for bit in (8, 16, 32, 64):
            theirs = jnp.where((turn & bit) != 0, pltpu.roll(theirs, bit, 1), theirs)
        halo = jnp.where(lane_group == j, jnp.where(own, mine, theirs), halo)
        return value, halo

    def settle(g, carry):
        halo_a = jnp.zeros((rows, LANES), jnp.float32)
        halo_b = jnp.zeros((rows, LANES), jnp.float32)
        for j in range(GROUP + 1):
            if j < GROUP:
                a, halo_a = fetch(g * GROUP + j, j, halo_a)
                b, halo_b = fetch((g + quarter) * GROUP + j, j, halo_b)
            else:
                a, b = halo_a, halo_b
            w_ref[g * packet + j] = a
            w_ref[(g + quarter) * packet + j] = b
            en[g * packet + j] = jnp.where(sub >= 4, a[top:], pltpu.roll(b[top:], 4, 0))
            ep[g * packet + j] = jnp.where(sub < 4, a[:8], pltpu.roll(b[:8], 4, 0))
        return carry

    lax.fori_loop(0, quarter, settle, 0)
    part = [pl.ds(g * packet, packet) for g in range(quarter)]
    edges = [
        (edge(en.at[part[g]], gn.at[part[g]], 1, 2 + 2 * g), edge(ep.at[part[g]], gp.at[part[g]], size - 1, 3 + 2 * g))
        for g in range(quarter)
    ]
    for down, up in edges:
        down.start()
        up.start()
    for g in range(quarter):
        edges[g][0].wait_recv()
        edges[g][1].wait_recv()
        for j in range(packet):
            down, up = gn[g * packet + j], gp[g * packet + j]
            h_ref[g * packet + j] = jnp.where(sub >= 4, down, up)
            h_ref[(g + quarter) * packet + j] = pltpu.roll(jnp.where(sub < 4, down, up), 4, 0)

    edge_down1.wait_send()
    edge_up1.wait_send()
    for down, up in edges:
        down.wait_send()
        up.wait_send()
    for to in range(2 * number):
        arrival(to).wait_send()


def exchange(index, tab, potentials):
    plan = PLANS[index]
    rows, columns = potentials.shape[1:]
    blocks = columns // LANES
    _, number = chunk_base(plan)
    groups = blocks // GROUP
    packet = GROUP + 1
    f32 = jnp.float32
    pairs = groups // 2 * packet
    edge = pltpu.VMEM((pairs, 8, LANES), f32)
    edge1 = pltpu.VMEM((8, columns // 2), f32)
    vmem = pl.BlockSpec(memory_space=pltpu.VMEM)
    return pl.pallas_call(
        functools.partial(exchange_kernel, plan),
        out_shape=(
            jax.ShapeDtypeStruct((groups * packet, rows, LANES), f32),
            jax.ShapeDtypeStruct((groups * packet, 8, LANES), f32),
            jax.ShapeDtypeStruct((8, columns), f32),
        ),
        in_specs=[pl.BlockSpec(memory_space=pltpu.SMEM), pl.BlockSpec(memory_space=pl.ANY)],
        out_specs=(vmem, vmem, vmem),
        scratch_shapes=[
            pltpu.VMEM((rows, columns), f32),
            pltpu.VMEM((rows, columns), f32),
            pltpu.VMEM((blocks, rows, LANES), f32),
            pltpu.VMEM((2 * plan[0] * packet, rows, LANES), f32),
            pltpu.VMEM((2 * number * packet, rows, LANES), f32),
            edge, edge, edge, edge,
            edge1, edge1, edge1, edge1,
            pltpu.SemaphoreType.DMA((2,)),
            pltpu.SemaphoreType.DMA((2 * number,)),
            pltpu.SemaphoreType.DMA((2 * number,)),
            pltpu.SemaphoreType.DMA((2 + groups,)),
            pltpu.SemaphoreType.DMA((2 + groups,)),
        ],
        compiler_params=pltpu.CompilerParams(
            collective_id=index, has_side_effects=True, vmem_limit_bytes=40 * 2**20
        ),
        name=f"exchange{index}",
    )(tab, potentials)


def lens_kernel(ratios, pot, h1, w, h, conv, shear, rot, disp):
    g = pl.program_id(0)
    rows = w.shape[1]
    columns = h1.shape[1]
    blocks = columns // LANES
    lane = iota((rows, LANES), 1)
    lane8 = iota((8, LANES), 1)
    sub = iota((8, LANES), 0)
    near_far, beta_one, beta_two = ratios[0], ratios[1], ratios[2]

    def across(x, t, k, where):
        ahead = pltpu.roll(jnp.where(where < k, t, x), LANES - k, 1)
        behind = pltpu.roll(jnp.where(where >= LANES - k, t, x), k, 1)
        return ahead, behind

    def slope_parts(x, t, where):
        a1, b1 = across(x, t, 1, where)
        a2, b2 = across(x, t, 2, where)
        return 8.0 * (a1 - b1) - (a2 - b2), a1 + b1, a2 + b2

    def second(x, s1, s2, s3, s4):
        return 16.0 * (s1 - s3) + 64.0 * s2 + s4 - 130.0 * x

    def along(a, b, e, k):
        plus = (
            pltpu.roll(jnp.where(sub < k, b, a), 8 - k, 0),
            pltpu.roll(jnp.where(sub < k, e, b), 8 - k, 0),
        )
        minus = (
            pltpu.roll(jnp.where(sub >= 8 - k, e, a), k, 0),
            pltpu.roll(jnp.where(sub >= 8 - k, a, b), k, 0),
        )
        return plus, minus

    def derive(x, t, e, te):
        slope_c, s1, s2 = slope_parts(x, t, lane)
        a3, b3 = across(x, t, 3, lane)
        a4, b4 = across(x, t, 4, lane)
        curve_cc = second(x, s1, s2, a3 + b3, a4 + b4)
        slope_c_e, _, _ = slope_parts(e, te, lane8)
        a, b = x[:8], x[8:]
        p1, m1 = along(a, b, e, 1)
        p2, m2 = along(a, b, e, 2)
        p3, m3 = along(a, b, e, 3)
        p4, m4 = along(a, b, e, 4)
        ca, cb = slope_c[:8], slope_c[8:]
        q1, n1 = along(ca, cb, slope_c_e, 1)
        q2, n2 = along(ca, cb, slope_c_e, 2)
        slope_r, curve_rr, curve_rc = [], [], []
        for i, mid in enumerate((a, b)):
            slope_r.append(8.0 * (p1[i] - m1[i]) - (p2[i] - m2[i]))
            curve_rr.append(second(mid, p1[i] + m1[i], p2[i] + m2[i], p3[i] + m3[i], p4[i] + m4[i]))
            curve_rc.append(8.0 * (q1[i] - n1[i]) - (q2[i] - n2[i]))
        join = functools.partial(jnp.concatenate, axis=0)
        return join(slope_r), slope_c, join(curve_rr), join(curve_rc), curve_cc

    one = 1.0 / 12.0
    two = 1.0 / 144.0
    for j in range(GROUP):
        c = g * GROUP + j
        before = lax.rem(c + (blocks - 1), blocks)
        after = lax.rem(c + 1, blocks)

        def at(i):
            return pl.ds(pl.multiple_of(i * LANES, LANES), LANES)

        near = derive(
            pot[0, :, at(c)],
            jnp.where(lane >= LANES // 2, pot[0, :, at(before)], pot[0, :, at(after)]),
            h1[:, at(c)],
            jnp.where(lane8 >= LANES // 2, h1[:, at(before)], h1[:, at(after)]),
        )
        back = (LANES - 8 * j - 4) % LANES
        far = derive(w[j], pltpu.roll(w[GROUP], back, 1), h[j], pltpu.roll(h[GROUP], back, 1))
        near_r, near_c, near_rr, near_rc, near_cc = near
        far_r, far_c, far_rr, far_rc, far_cc = far
        near_rr, near_rc, near_cc = near_rr * two, near_rc * two, near_cc * two
        inner_rr = 1.0 - near_far * near_rr
        inner_cc = 1.0 - near_far * near_cc
        inner_rc = -near_far * near_rc
        scale = 0.5 * two * beta_two
        half_one = 0.5 * beta_one
        chain_rr = far_rr * inner_rr + far_rc * inner_rc
        chain_cc = far_rc * inner_rc + far_cc * inner_cc
        chain_rc = far_rr * inner_rc + far_rc * inner_cc
        chain_cr = far_rc * inner_rr + far_cc * inner_rc
        spot = pl.ds(j * LANES, LANES)
        conv[:, spot] = half_one * (near_rr + near_cc) + scale * (chain_rr + chain_cc)
        shear[0, :, spot] = half_one * (near_cc - near_rr) + scale * (chain_cc - chain_rr)
        shear[1, :, spot] = beta_one * near_rc + scale * (chain_rc + chain_cr)
        rot[:, spot] = scale * (chain_cr - chain_rc)
        disp[0, :, spot] = (one * beta_one) * near_r + (one * beta_two) * far_r
        disp[1, :, spot] = (one * beta_one) * near_c + (one * beta_two) * far_c


def lens(ratios, potentials, h1, w, h):
    rows, columns = potentials.shape[1:]
    packet = GROUP + 1
    wide = GROUP * LANES
    f32 = jnp.float32
    flat = jax.ShapeDtypeStruct((rows, columns), f32)
    pair = jax.ShapeDtypeStruct((2, rows, columns), f32)
    flat_spec = pl.BlockSpec((rows, wide), lambda g: (0, g))
    pair_spec = pl.BlockSpec((2, rows, wide), lambda g: (0, 0, g))
    return pl.pallas_call(
        lens_kernel,
        grid=(columns // wide,),
        out_shape=(flat, pair, flat, pair),
        in_specs=[
            pl.BlockSpec(memory_space=pltpu.SMEM),
            pl.BlockSpec((1, rows, columns), lambda g: (0, 0, 0)),
            pl.BlockSpec((8, columns), lambda g: (0, 0)),
            pl.BlockSpec((packet, rows, LANES), lambda g: (g, 0, 0)),
            pl.BlockSpec((packet, 8, LANES), lambda g: (g, 0, 0)),
        ],
        out_specs=(flat_spec, pair_spec, flat_spec, pair_spec),
        compiler_params=pltpu.CompilerParams(vmem_limit_bytes=40 * 2**20),
        name="lens",
    )(ratios, potentials, h1, w, h)


def per_device(potentials, ratios, row_offset, col_offset):
    blocks = row_offset.shape[0]
    vmem = pl.BlockSpec(memory_space=pltpu.VMEM)
    tab = pl.pallas_call(
        table_kernel,
        out_shape=jax.ShapeDtypeStruct((8, blocks), jnp.int32),
        in_specs=[vmem, vmem],
        out_specs=vmem,
        name="table",
    )(row_offset.reshape(1, blocks), col_offset.reshape(1, blocks))
    w, h, h1 = lax.cond(
        tab[7, 0] == 0,
        functools.partial(exchange, 0),
        functools.partial(exchange, 1),
        tab,
        potentials,
    )
    return lens(ratios, potentials, h1, w, h)


def solution(mesh):
    return jax.shard_map(
        per_device,
        mesh=mesh,
        in_specs=(P("cosmo", "row", None), P("cosmo"), P("cosmo"), P("cosmo")),
        out_specs=(
            P(("cosmo", "row"), None),
            P(None, ("cosmo", "row"), None),
            P(("cosmo", "row"), None),
            P(None, ("cosmo", "row"), None),
        ),
        check_vma=False,
    )
```

time: 421 us -> 86.9 us (0.21)
  the two profiles are of different devices: /device:TPU:543 before, /device:TPU:527 now
where the time goes in v1:
time: 86.9 us; the launch traced here: 86.7 us
  Pallas kernels  84.9 us (98%)
  between operations  1.31 us (2%)
    pallas_call x1, Pallas kernels, exchange(): pl.pallas_call(functools.partial(exchange_kernel, plan), out_shape=(jax.S...  68 us
    pallas_call x1, Pallas kernels, lens(): pl.pallas_call(lens_kernel, grid=(columns // wide,), out_shape=(flat, pai...  15.9 us

profile of v1, /device:TPU:527, one launch (start us, length us, event | category | flops | bytes accessed | tf_op | source)
XLA Modules:
  0.0 86.7 jit_solution(712866642064975398)
XLA Ops:
  0.6 1.0 %table.1 = s32[8,128]{1,0:T(8,128)S(1)} custom-call(s32[1,128]{1,0:T(1,128)} %bitcast.3, s32[1,128]{1,0:T(1,128)} %bitcast.4), custom_call_target="tpu_custom_call" | custom-call | tf_op jit(solution)/shard_map/table/pallas_call | solution.py:467
  1.6 0.5 slice.3
  2.8 0.0 copy-start
  2.8 68.0 %conditional.1 = ((f32[136,16,128]{2,1,0:T(8,128)S(1)}, f32[136,8,128]{2,1,0:T(8,128)S(1)}, f32[8,16384]{1,0:T(8,128)S(1)})) conditional(s32[]{:T(128)} %bitcast.2, (s32[8,128]{1,0:T(8,128)S(1)}, f32[2,16,16384]{2,1,0:T(8,128)}) %tuple.13, (s32[8,128]{1,0:T(8,128)S(1)}, f32[2,16,16384]{2,1,0:T(8,128)}) %tuple.13), branch_computations={%region_0.0_spmd, %region_1.0_spmd} | conditional | bytes 8 | solution.py:474
  2.8 68.0 %exchange0.1 = (f32[136,16,128]{2,1,0:T(8,128)S(1)}, f32[136,8,128]{2,1,0:T(8,128)S(1)}, f32[8,16384]{1,0:T(8,128)S(1)}) custom-call(s32[8,128]{1,0:T(8,128)S(1)} %get-tuple-element.10.tab, f32[2,16,16384]{2,1,0:T(8,128)} %get-tuple-element.11.pot), custom_call_target="tpu_custom_call" | custom-call | tf_op jit(solution)/shard_map/cond/branch_1_fun/exchange0/pallas_call | solution.py:313
  70.8 0.0 copy-done
  70.8 15.9 %lens.1 = (f32[16,16384]{1,0:T(8,128)}, f32[2,16,16384]{2,1,0:T(8,128)}, f32[16,16384]{1,0:T(8,128)}, f32[2,16,16384]{2,1,0:T(8,128)}) custom-call(f32[3]{0:T(128)S(1)} %copy-done, f32[2,16,16384]{2,1,0:T(8,128)} %pot.1, f32[8,16384]{1,0:T(8,128)S(1)} %get-tuple-element.19.h1, f32[136,16,128]{2,1,0:T(8,128)S(1)} %get-tuple-element.20.w, ...), custom_call_target="tpu_custom_call" | custom-call | tf_op jit(solution)/shard_map/lens/pallas_call | solution.py:447
Async XLA Ops:
  2.8 68.0 %copy-start = (f32[3]{0:T(128)S(1)}, f32[3]{0:T(128)}, u32[]{:S(2)}) copy-start(f32[3]{0:T(128)} %ratios.1) | copy-start | bytes 40

commit v2 on v0

v2 whole, which is shorter than its diff:
```python
import functools

import jax
import jax.numpy as jnp
from jax import lax
from jax.experimental import pallas as pl
from jax.experimental.pallas import tpu as pltpu
from jax.sharding import PartitionSpec as P

RB = 8
LANES = 128
HALF = RB // 2
GROUP = 16
PACKET = GROUP + 1
EDGE = 4
MESH = pl.DeviceIdType.MESH

PLANS = (((4, 3, 2, 1), (3, 6, 8)), ((8, 8, 8, 4), (8,)))
STORES = ((0, 1), (2,), (3,))


def chunk_base(hops):
    base, total = [], 0
    for count in hops:
        base.append(total)
        total += count
    return base, total


def store_of(hop):
    return [i for i, members in enumerate(STORES) if hop in members][0]


def store_size(hops, i):
    return sum(hops[hop] for hop in STORES[i])


def store_base(hops, hop):
    members = STORES[store_of(hop)]
    return sum(hops[other] for other in members if other < hop)


def iota(shape, dim):
    return lax.broadcasted_iota(jnp.int32, shape, dim)


def table_kernel(row_ref, col_ref, tab_ref):
    blocks = row_ref.shape[1]
    square = (blocks, blocks)
    f32 = jnp.float32
    row = row_ref[...].astype(f32)
    lane_f = iota((1, blocks), 1).astype(f32)
    source = lane_f + col_ref[...].astype(f32)
    source = jnp.where(source >= blocks, source - blocks, source)
    sub2 = iota(square, 0)
    lane2 = iota(square, 1)
    lane2_f = lane2.astype(f32)

    def spread(v):
        return jnp.broadcast_to(v, square)

    def column(v):
        return spread(jnp.sum(jnp.where(sub2 == lane2, spread(v), 0.0), axis=1, keepdims=True))

    def total(v):
        return jnp.sum(v, axis=1, keepdims=True)

    def down(v):
        return jnp.sum(v, axis=0, keepdims=True)

    halfway = (row == HALF).astype(f32)
    dist = jnp.where(row <= HALF, row, RB - row)
    n_half = total(halfway)
    load_a = total(jnp.where(row < HALF, row, 0.0))
    load_b = total(jnp.where(row > HALF, RB - row, 0.0))
    take_a = jnp.clip(jnp.floor((load_b + HALF * n_half - load_a) / (2 * HALF) + 0.5), 0.0, n_half)
    rank_half = down(jnp.where(sub2 < lane2, column(halfway), 0.0))
    way = jnp.where(row == 0, 0.0, jnp.where(row < HALF, 1.0, 2.0))
    way = jnp.where((row == HALF) & (rank_half < take_a), 1.0, way)
    big = 4096.0
    key = way * big + (HALF - dist) * blocks + lane_f
    key_c = column(key)
    slot = down(((key_c < spread(key)) & (key_c >= spread(way * big))).astype(f32))
    near = dist * blocks + lane_f
    near_c = column(near)
    place = down((near_c < spread(near)).astype(f32))

    fits = jnp.ones((1, 1), f32)
    hops, ends = PLANS[0]
    for hop, count in enumerate(hops):
        for w in (1.0, 2.0):
            need = total(((way == w) & (dist > hop)).astype(f32))
            fits = jnp.where(need > count * GROUP, 0.0, fits)
    for end, reach in zip(ends, (2, 3, 4)):
        fits = jnp.where(total((dist <= reach).astype(f32)) < end * GROUP, 0.0, fits)
    fits = jnp.where(total((dist == 0).astype(f32)) > ends[0] * GROUP, 0.0, fits)

    chunk = jnp.floor(slot / GROUP)
    within = slot - chunk * GROUP
    spot = []
    for hops, _ in PLANS:
        at = jnp.zeros((1, blocks), f32)
        for hop in range(HALF):
            other = jnp.where(way == 2.0, float(store_size(hops, store_of(hop))), 0.0)
            at = jnp.where(dist == hop + 1, other + float(store_base(hops, hop)), at)
        spot.append(at + chunk)
    spot = jnp.where(fits > 0, spot[0], spot[1])
    spot = jnp.where(way == 0, 0.0, spot)
    within = jnp.where(way == 0, 0.0, within)
    kind = jnp.zeros((1, blocks), f32)
    for hop in range(HALF):
        kind = jnp.where(dist == hop + 1, float(store_of(hop) + 1), kind)

    slot_c, way_c, source_c, place_c = column(slot), column(way), column(source), column(place)
    here = slot_c == lane2_f
    send = [down(jnp.where(here & (way_c == w), source_c, 0.0)) for w in (1.0, 2.0)]
    there = place_c == lane2_f

    def ordered(v):
        return down(jnp.where(there, column(v), 0.0))

    at = ordered(spot)
    inside = ordered(within)
    turn = 8.0 * (lane_f - GROUP * jnp.floor(lane_f / GROUP) - inside)
    turn = jnp.where(turn < 0, turn + LANES, turn)
    rows = [
        send[0],
        send[1],
        at * PACKET + inside,
        at * PACKET + GROUP,
        turn,
        down(jnp.where(there, source_c, 0.0)),
        ordered(kind),
        down(jnp.where(there, sub2.astype(f32), 0.0)),
        place,
        spread(1.0 - fits)[:1],
    ]
    rows += [jnp.zeros((1, blocks), f32)] * (16 - len(rows))
    tab_ref[...] = jnp.concatenate(rows, axis=0).astype(jnp.int32)


def exchange_kernel(plan, tab, ratios, pot, out, p1, p2, tiles, sent, got_a, got_b, got_c, v1, v2, near, c1s, ccs,
                    local_sem, send_sem, recv_sem, edge_send, edge_recv):
    hops, ends = plan
    base, number = chunk_base(hops)
    stores = (got_a, got_b, got_c)
    size = lax.axis_size("row")
    stride = size // RB
    me = lax.axis_index("row")
    blocks = tiles.shape[0]
    rows = tiles.shape[1]
    tall = rows + 2 * EDGE
    first = hops[0]
    single = len(ends) == 1

    load2 = pltpu.make_async_copy(pot.at[1], p2, local_sem.at[0])
    load1 = pltpu.make_async_copy(pot.at[0], p1, local_sem.at[1])
    load2.start()
    load1.start()
    barrier = pltpu.get_barrier_semaphore()
    for by in (stride, size - stride, 1, size - 1):
        pl.semaphore_signal(barrier, inc=1, device_id={"row": lax.rem(me + by, size)}, device_id_type=MESH)

    lane = iota((rows, LANES), 1)
    lane_group = lane // 8
    lane_t = iota((tall, LANES), 1)

    def split(source, put):
        def body(i, carry):
            for j in range(GROUP):
                b = i * GROUP + j
                put(b, source[:, pl.ds(pl.multiple_of(b * LANES, LANES), LANES)])
            return carry

        lax.fori_loop(0, blocks // GROUP, body, 0)

    def put_tile(b, value):
        tiles[b] = value

    def put_v1(b, value):
        v1[b, EDGE : EDGE + rows, :] = value

    def sides(s):
        before = tiles[lax.rem(s + (blocks - 1), blocks)]
        after = tiles[lax.rem(s + 1, blocks)]
        return jnp.where(lane >= LANES // 2, before, after)

    def pack(i):
        way = lax.rem(i, 2)
        chunk = i // 2
        halo = jnp.zeros((rows, LANES), jnp.float32)
        for j in range(GROUP):
            s = tab[way, chunk * GROUP + j]
            sent[i * PACKET + j] = tiles[s]
            halo = jnp.where(lane_group == j, pltpu.roll(sides(s), (8 * j + 4) % LANES, 1), halo)
        sent[i * PACKET + GROUP] = halo

    def first_copy(i):
        way = lax.rem(i, 2)
        to = way * number + i // 2
        land = way * store_size(hops, 0) + i // 2
        return pltpu.make_async_remote_copy(
            src_ref=sent.at[pl.ds(i * PACKET, PACKET)],
            dst_ref=got_a.at[pl.ds(land * PACKET, PACKET)],
            send_sem=send_sem.at[to],
            recv_sem=recv_sem.at[to],
            device_id={"row": lax.rem(me + jnp.where(way == 0, size - stride, stride), size)},
            device_id_type=MESH,
        )

    def piece(way, hop, c):
        where = store_of(hop)
        at = way * store_size(hops, where) + store_base(hops, hop) + c
        return stores[where].at[pl.ds(at * PACKET, PACKET)]

    def relay(way, hop, c):
        to = way * number + base[hop] + c
        return pltpu.make_async_remote_copy(
            src_ref=piece(way, hop - 1, c),
            dst_ref=piece(way, hop, c),
            send_sem=send_sem.at[to],
            recv_sem=recv_sem.at[to],
            device_id={"row": lax.rem(me + (size - stride if way == 0 else stride), size)},
            device_id_type=MESH,
        )

    def arrival(way, hop, c):
        to = way * number + base[hop] + c
        here = piece(way, hop, c)
        return pltpu.make_async_remote_copy(
            src_ref=here, dst_ref=here, send_sem=send_sem.at[to], recv_sem=recv_sem.at[to],
            device_id={"row": lax.rem(me + stride, size)}, device_id_type=MESH,
        )

    def edges(ref, begin, end, at):
        span = pl.ds(begin, end - begin)
        pair = []
        for k, (src, dst, by) in enumerate(((rows, 0, 1), (EDGE, EDGE + rows, size - 1))):
            pair.append(
                pltpu.make_async_remote_copy(
                    src_ref=ref.at[span, src : src + EDGE, :],
                    dst_ref=ref.at[span, dst : dst + EDGE, :],
                    send_sem=edge_send.at[2 * at + k],
                    recv_sem=edge_recv.at[2 * at + k],
                    device_id={"row": lax.rem(me + by, size)},
                    device_id_type=MESH,
                )
            )
        return pair

    load2.wait()
    split(p2, put_tile)
    pack(0)
    pl.semaphore_wait(barrier, 4)

    def step(i, carry):
        pack(i)
        first_copy(i - 1).start()
        return carry

    lax.fori_loop(1, 2 * first, step, 0)
    first_copy(2 * first - 1).start()

    load1.wait()
    split(p1, put_v1)
    edges1 = edges(v1, 0, blocks, 0)
    for copy in edges1:
        copy.start()

    near_far, beta_one, beta_two = ratios[0], ratios[1], ratios[2]
    one = 1.0 / 12.0
    two = 1.0 / 144.0

    def second(x, s1, s2, s3, s4):
        return 16.0 * (s1 - s3) + 64.0 * s2 + s4 - 130.0 * x

    def derive(ref, f, t, j):
        x = ref[f]
        ahead = [pltpu.roll(jnp.where(lane_t < k, t, x), LANES - k, 1) for k in range(1, 5)]
        behind = [pltpu.roll(jnp.where(lane_t >= LANES - k, t, x), k, 1) for k in range(1, 5)]
        c1s[j] = 8.0 * (ahead[0] - behind[0]) - (ahead[1] - behind[1])
        ccs[j] = second(x, *[a + b for a, b in zip(ahead, behind)])

        def tap(k):
            return ref[f, EDGE + k : EDGE + k + rows, :]

        def tap_c(k):
            return c1s[j, EDGE + k : EDGE + k + rows, :]

        up = [tap(k) for k in range(1, 5)]
        low = [tap(-k) for k in range(1, 5)]
        slope_r = 8.0 * (up[0] - low[0]) - (up[1] - low[1])
        curve_rr = second(tap(0), *[a + b for a, b in zip(up, low)])
        curve_rc = 8.0 * (tap_c(1) - tap_c(-1)) - (tap_c(2) - tap_c(-2))
        curve_cc = ccs[j, EDGE : EDGE + rows, :]
        return slope_r, tap_c(0), curve_rr, curve_rc, curve_cc

    def near_group(g):
        for j in range(GROUP):
            b = g * GROUP + j
            before = v1[lax.rem(b + (blocks - 1), blocks)]
            after = v1[lax.rem(b + 1, blocks)]
            slope_r, slope_c, curve_rr, curve_rc, curve_cc = derive(v1, b, jnp.where(lane_t >= LANES // 2, before, after), j)
            near[b, 0 * rows : 1 * rows, :] = two * (curve_rr + curve_cc)
            near[b, 1 * rows : 2 * rows, :] = two * (curve_cc - curve_rr)
            near[b, 2 * rows : 3 * rows, :] = (2.0 * two) * curve_rc
            near[b, 3 * rows : 4 * rows, :] = (one * beta_one) * slope_r
            near[b, 4 * rows : 5 * rows, :] = (one * beta_one) * slope_c

    def near_groups(begin, end):
        def body(g, carry):
            near_group(g)
            return carry

        lax.fori_loop(begin, end, body, 0)

    def gather(begin, end, kinds):
        def body(g, carry):
            halo = jnp.zeros((rows, LANES), jnp.float32)
            for j in range(GROUP):
                f = g * GROUP + j
                kind = jnp.full((rows, LANES), tab[6, f], jnp.int32)
                value = cols = None
                for k in kinds:
                    if k == 0:
                        s = tab[5, f]
                        v, c = tiles[s], pltpu.roll(sides(s), (8 * j + 4) % LANES, 1)
                    else:
                        ref = stores[k - 1]
                        limit = ref.shape[0] - 1
                        v = ref[jnp.minimum(tab[2, f], limit)]
                        c = ref[jnp.minimum(tab[3, f], limit)]
                        c = pltpu.roll(c, tab[4, f], 1)
                    value = v if value is None else jnp.where(kind == k, v, value)
                    cols = c if cols is None else jnp.where(kind == k, c, cols)
                halo = jnp.where(lane_group == j, cols, halo)
                v2[g * PACKET + j, EDGE : EDGE + rows, :] = value
            v2[g * PACKET + GROUP, EDGE : EDGE + rows, :] = halo
            return carry

        lax.fori_loop(begin, end, body, 0)

    scale = 0.5 * two * beta_two
    half_far = 0.5 * near_far
    half_one = 0.5 * beta_one
    slope_scale = one * beta_two

    def combine(begin, end):
        def body(g, carry):
            halo = v2[g * PACKET + GROUP]
            for j in range(GROUP):
                f = g * GROUP + j
                t = pltpu.roll(halo, (LANES - 8 * j - 4) % LANES, 1)
                far_r, far_c, far_rr, far_rc, far_cc = derive(v2, g * PACKET + j, t, j)
                n = near[tab[7, f]]
                n_sum, n_diff, n_rc2, n_r, n_c = (n[k * rows : (k + 1) * rows] for k in range(5))
                s = scale * (far_rr + far_cc)
                d = scale * (far_cc - far_rr)
                r = scale * far_rc
                d_half = half_far * d
                r_far = near_far * r
                rest = half_one - half_far * s
                out[f, 0 * rows : 1 * rows, :] = s + n_sum * rest - d_half * n_diff - r_far * n_rc2
                out[f, 1 * rows : 2 * rows, :] = d + n_diff * rest - d_half * n_sum
                out[f, 2 * rows : 3 * rows, :] = (r + r) + n_rc2 * rest - r_far * n_sum
                out[f, 3 * rows : 4 * rows, :] = r_far * n_diff - n_rc2 * d_half
                out[f, 4 * rows : 5 * rows, :] = n_r + slope_scale * far_r
                out[f, 5 * rows : 6 * rows, :] = n_c + slope_scale * far_c
            return carry

        lax.fori_loop(begin, end, body, 0)

    def forward(hop, c):
        for way in range(2):
            arrival(way, hop - 1, c).wait_recv()
            relay(way, hop, c).start()

    def land(hop):
        for c in range(hops[hop + 1] if hop + 1 < HALF else 0, hops[hop]):
            for way in range(2):
                arrival(way, hop, c).wait_recv()

    groups = blocks // GROUP
    relays = [(hop, c) for hop in range(1, HALF) for c in range(hops[hop])]
    late = [(hop, c) for hop, c in relays if hop == HALF - 1]
    early = [pair for pair in relays if pair not in late]
    share = max(1, -(-groups // (len(early) - 1)))
    done = 0
    for i, (hop, c) in enumerate(early):
        forward(hop, c)
        if i == 0:
            for copy in edges1:
                copy.wait_recv()
        upto = min(groups, done + share)
        if upto > done:
            near_groups(done, upto)
        done = upto
    if done < groups:
        near_groups(done, groups)

    bounds = [0] + list(ends)
    moved = [edges(v2, bounds[p] * PACKET, bounds[p + 1] * PACKET, 1 + p) for p in range(len(ends))]

    def begin_phase(p, kinds):
        gather(bounds[p], bounds[p + 1], kinds)
        for copy in moved[p]:
            copy.start()

    def end_phase(p):
        for copy in moved[p]:
            copy.wait_recv()
        combine(bounds[p], bounds[p + 1])

    land(0)
    land(1)
    if single:
        for hop, c in late:
            forward(hop, c)
        land(2)
        land(3)
        begin_phase(0, (0, 1, 2, 3))
        end_phase(0)
    else:
        begin_phase(0, (0, 1))
        for hop, c in late:
            forward(hop, c)
        end_phase(0)
        land(2)
        begin_phase(1, (1, 2))
        land(3)
        begin_phase(2, (1, 2, 3))
        end_phase(1)
        end_phase(2)

    for copy in edges1:
        copy.wait_send()
    for pair in moved:
        for copy in pair:
            copy.wait_send()
    for way in range(2):
        for hop in range(HALF):
            for c in range(hops[hop]):
                arrival(way, hop, c).wait_send()


def exchange(index, tab, ratios, potentials):
    plan = PLANS[index]
    hops, ends = plan
    rows, columns = potentials.shape[1:]
    blocks = columns // LANES
    _, number = chunk_base(hops)
    packets = blocks // GROUP * PACKET
    tall = rows + 2 * EDGE
    f32 = jnp.float32
    smem = pl.BlockSpec(memory_space=pltpu.SMEM)
    return pl.pallas_call(
        functools.partial(exchange_kernel, plan),
        out_shape=jax.ShapeDtypeStruct((blocks, 6 * rows, LANES), f32),
        in_specs=[smem, smem, pl.BlockSpec(memory_space=pl.ANY)],
        out_specs=pl.BlockSpec(memory_space=pltpu.VMEM),
        scratch_shapes=[
            pltpu.VMEM((rows, columns), f32),
            pltpu.VMEM((rows, columns), f32),
            pltpu.VMEM((blocks, rows, LANES), f32),
            pltpu.VMEM((2 * hops[0] * PACKET, rows, LANES), f32),
            *[pltpu.VMEM((2 * store_size(hops, i) * PACKET, rows, LANES), f32) for i in range(len(STORES))],
            pltpu.VMEM((blocks, tall, LANES), f32),
            pltpu.VMEM((packets, tall, LANES), f32),
            pltpu.VMEM((blocks, 5 * rows, LANES), f32),
            pltpu.VMEM((GROUP, tall, LANES), f32),
            pltpu.VMEM((GROUP, tall, LANES), f32),
            pltpu.SemaphoreType.DMA((2,)),
            pltpu.SemaphoreType.DMA((2 * number,)),
            pltpu.SemaphoreType.DMA((2 * number,)),
            pltpu.SemaphoreType.DMA((2 + 2 * len(ends),)),
            pltpu.SemaphoreType.DMA((2 + 2 * len(ends),)),
        ],
        compiler_params=pltpu.CompilerParams(
            collective_id=index, has_side_effects=True, vmem_limit_bytes=30 * 2**20
        ),
        name=f"exchange{index}",
    )(tab, ratios, potentials)


def arrange_kernel(tab, fields, conv, shear, rot, disp):
    g = pl.program_id(0)
    rows = conv.shape[0]
    for j in range(GROUP):
        value = fields[tab[8, g * GROUP + j]]
        part = [value[k * rows : (k + 1) * rows] for k in range(6)]
        spot = slice(j * LANES, (j + 1) * LANES)
        conv[:, spot] = part[0]
        shear[0, :, spot] = part[1]
        shear[1, :, spot] = part[2]
        rot[:, spot] = part[3]
        disp[0, :, spot] = part[4]
        disp[1, :, spot] = part[5]


def arrange(tab, fields, rows):
    columns = fields.shape[0] * LANES
    wide = GROUP * LANES
    f32 = jnp.float32
    flat = jax.ShapeDtypeStruct((rows, columns), f32)
    pair = jax.ShapeDtypeStruct((2, rows, columns), f32)
    flat_spec = pl.BlockSpec((rows, wide), lambda g: (0, g))
    pair_spec = pl.BlockSpec((2, rows, wide), lambda g: (0, 0, g))
    return pl.pallas_call(
        arrange_kernel,
        grid=(columns // wide,),
        out_shape=(flat, pair, flat, pair),
        in_specs=[pl.BlockSpec(memory_space=pltpu.SMEM), pl.BlockSpec(memory_space=pltpu.VMEM)],
        out_specs=(flat_spec, pair_spec, flat_spec, pair_spec),
        compiler_params=pltpu.CompilerParams(vmem_limit_bytes=16 * 2**20),
        name="arrange",
    )(tab, fields)


def per_device(potentials, ratios, row_offset, col_offset):
    blocks = row_offset.shape[0]
    vmem = pl.BlockSpec(memory_space=pltpu.VMEM)
    tab = pl.pallas_call(
        table_kernel,
        out_shape=jax.ShapeDtypeStruct((16, blocks), jnp.int32),
        in_specs=[vmem, vmem],
        out_specs=vmem,
        compiler_params=pltpu.CompilerParams(vmem_limit_bytes=4 * 2**20),
        name="table",
    )(row_offset.reshape(1, blocks), col_offset.reshape(1, blocks))
    def run(index, tab, ratios, potentials):
        return arrange(tab, exchange(index, tab, ratios, potentials), potentials.shape[1])

    return lax.cond(
        tab[9, 0] == 0, functools.partial(run, 0), functools.partial(run, 1), tab, ratios, potentials
    )


def solution(mesh):
    return jax.shard_map(
        per_device,
        mesh=mesh,
        in_specs=(P("cosmo", "row", None), P("cosmo"), P("cosmo"), P("cosmo")),
        out_specs=(
            P(("cosmo", "row"), None),
            P(None, ("cosmo", "row"), None),
            P(("cosmo", "row"), None),
            P(None, ("cosmo", "row"), None),
        ),
        check_vma=False,
    )
```

time: 421 us -> 74.6 us (0.18)
  the two profiles are of different devices: /device:TPU:543 before, /device:TPU:528 now
where the time goes in v2:
time: 74.6 us; the launch traced here: 74.4 us
  Pallas kernels  71.1 us (95%)
  local copies, waits for them, and re-layouts  1.82 us (2%)
  between operations  1.3 us (2%)
    pallas_call x1, Pallas kernels, exchange(): pl.pallas_call(functools.partial(exchange_kernel, plan), out_shape=jax.Sh...  65.9 us
    pallas_call x1, Pallas kernels, arrange(): pl.pallas_call(arrange_kernel, grid=(columns // wide,), out_shape=(flat,...  4.81 us

profile of v2, /device:TPU:528, one launch (start us, length us, event | category | flops | bytes accessed | tf_op | source)
XLA Modules:
  0.0 74.4 jit_solution(13483328914512044361)
XLA Ops:
  0.6 0.0 copy-start
  0.6 0.6 copy-done
  1.3 0.0 copy-start.1
  1.3 0.7 copy-done.1
  1.9 0.4 table.1
  2.3 0.5 slice.4
  3.5 70.9 %conditional.1 = ((f32[16,16384]{1,0:T(8,128)}, f32[2,16,16384]{2,1,0:T(8,128)}, f32[16,16384]{1,0:T(8,128)}, f32[2,16,16384]{2,1,0:T(8,128)})) conditional(s32[]{:T(128)} %bitcast.2, (s32[16,128]{1,0:T(8,128)S(1)}, f32[3]{0:T(128)}, f32[2,16,16384]{2,1,0:T(8,128)}) %tuple.13, (s32[16,128]{1,0:T(8,128)S(1)}, f32[3]{0:T(128)}, ...), branch_computations={%region_0.0_spmd, %region_1.0_spmd} | conditional | bytes 8 | solution.py:533
  3.7 65.9 %exchange0.1.fields = f32[128,96,128]{2,1,0:T(8,128)S(1)} custom-call(s32[16,128]{1,0:T(8,128)S(1)} %get-tuple-element.15.tab, f32[3]{0:T(128)} %get-tuple-element.39.ratios, f32[2,16,16384]{2,1,0:T(8,128)} %get-tuple-element.41.pot), custom_call_target="tpu_custom_call" | custom-call | tf_op jit(solution)/shard_map/cond/branch_1_fun/exchange0/pallas_call | solution.py:456
  69.6 4.8 %arrange.3 = (f32[16,16384]{1,0:T(8,128)}, f32[2,16,16384]{2,1,0:T(8,128)}, f32[16,16384]{1,0:T(8,128)}, f32[2,16,16384]{2,1,0:T(8,128)}) custom-call(s32[16,128]{1,0:T(8,128)S(1)} %get-tuple-element.15.tab, f32[128,96,128]{2,1,0:T(8,128)S(1)} %exchange0.1.fields), custom_call_target="tpu_custom_call" | custom-call | tf_op jit(solution)/shard_map/cond/branch_1_fun/arrange/pallas_call | solution.py:508
Async XLA Ops:
  0.6 0.7 copy-start
  1.3 0.7 copy-start.1

commit v3 on v2

--- a/solution.py
+++ b/solution.py
@@ -15,8 +15,12 @@
 EDGE = 4
 MESH = pl.DeviceIdType.MESH
 
-PLANS = (((4, 3, 2, 1), (3, 6, 8)), ((8, 8, 8, 4), (8,)))
-STORES = ((0, 1), (2,), (3,))
+PLANS = (
+    ((4, 3, 2, 1), ((2, 0, 1), (4, 1, 2), (6, 2, 3), (8, 3, 4))),
+    ((4, 3, 2, 1), ((3, 0, 2), (6, 1, 3), (8, 2, 4))),
+    ((8, 8, 8, 4), ((8, 0, 4),)),
+)
+STORES = ((0,), (1,), (2,), (3,))
 
 
 def chunk_base(hops):
@@ -85,15 +89,23 @@
     near_c = column(near)
     place = down((near_c < spread(near)).astype(f32))
 
-    fits = jnp.ones((1, 1), f32)
-    hops, ends = PLANS[0]
-    for hop, count in enumerate(hops):
-        for w in (1.0, 2.0):
-            need = total(((way == w) & (dist > hop)).astype(f32))
-            fits = jnp.where(need > count * GROUP, 0.0, fits)
-    for end, reach in zip(ends, (2, 3, 4)):
-        fits = jnp.where(total((dist <= reach).astype(f32)) < end * GROUP, 0.0, fits)
-    fits = jnp.where(total((dist == 0).astype(f32)) > ends[0] * GROUP, 0.0, fits)
+    def fitting(plan):
+        hops, phases = plan
+        fits = jnp.ones((1, 1), f32)
+        for hop, count in enumerate(hops):
+            for w in (1.0, 2.0):
+                fits = jnp.where(total(((way == w) & (dist > hop)).astype(f32)) > count * GROUP, 0.0, fits)
+        start = 0
+        for end, least, reach in phases:
+            fits = jnp.where(total((dist < least).astype(f32)) > start * GROUP, 0.0, fits)
+            fits = jnp.where(total((dist <= reach).astype(f32)) < end * GROUP, 0.0, fits)
+            start = end
+        return fits
+
+    fits = [fitting(plan) for plan in PLANS[:-1]]
+    choice = jnp.full((1, 1), float(len(PLANS) - 1), f32)
+    for i in reversed(range(len(PLANS) - 1)):
+        choice = jnp.where(fits[i] > 0, float(i), choice)
 
     chunk = jnp.floor(slot / GROUP)
     within = slot - chunk * GROUP
@@ -104,13 +116,9 @@
             other = jnp.where(way == 2.0, float(store_size(hops, store_of(hop))), 0.0)
             at = jnp.where(dist == hop + 1, other + float(store_base(hops, hop)), at)
         spot.append(at + chunk)
-    spot = jnp.where(fits > 0, spot[0], spot[1])
+    spot = functools.reduce(lambda rest, i: jnp.where(choice == i, spot[i], rest), range(len(PLANS) - 1), spot[-1])
     spot = jnp.where(way == 0, 0.0, spot)
     within = jnp.where(way == 0, 0.0, within)
-    kind = jnp.zeros((1, blocks), f32)
-    for hop in range(HALF):
-        kind = jnp.where(dist == hop + 1, float(store_of(hop) + 1), kind)
-
     slot_c, way_c, source_c, place_c = column(slot), column(way), column(source), column(place)
     here = slot_c == lane2_f
     send = [down(jnp.where(here & (way_c == w), source_c, 0.0)) for w in (1.0, 2.0)]
@@ -121,7 +129,8 @@
 
     at = ordered(spot)
     inside = ordered(within)
-    turn = 8.0 * (lane_f - GROUP * jnp.floor(lane_f / GROUP) - inside)
+    kind = ordered(dist)
+    turn = 8.0 * (lane_f - GROUP * jnp.floor(lane_f / GROUP) - inside) + jnp.where(kind == 0, 4.0, 0.0)
     turn = jnp.where(turn < 0, turn + LANES, turn)
     rows = [
         send[0],
@@ -130,20 +139,20 @@
         at * PACKET + GROUP,
         turn,
         down(jnp.where(there, source_c, 0.0)),
-        ordered(kind),
+        kind,
         down(jnp.where(there, sub2.astype(f32), 0.0)),
         place,
-        spread(1.0 - fits)[:1],
+        spread(choice)[:1],
     ]
     rows += [jnp.zeros((1, blocks), f32)] * (16 - len(rows))
     tab_ref[...] = jnp.concatenate(rows, axis=0).astype(jnp.int32)
 
 
-def exchange_kernel(plan, tab, ratios, pot, out, p1, p2, tiles, sent, got_a, got_b, got_c, v1, v2, near, c1s, ccs,
+def exchange_kernel(plan, tab, ratios, pot, out, p1, p2, tiles, sent, got_a, got_b, got_c, got_d, v1, v2, near, c1s,
                     local_sem, send_sem, recv_sem, edge_send, edge_recv):
-    hops, ends = plan
+    hops, phases = plan
     base, number = chunk_base(hops)
-    stores = (got_a, got_b, got_c)
+    stores = (got_a, got_b, got_c, got_d)
     size = lax.axis_size("row")
     stride = size // RB
     me = lax.axis_index("row")
@@ -151,7 +160,6 @@
     rows = tiles.shape[1]
     tall = rows + 2 * EDGE
     first = hops[0]
-    single = len(ends) == 1
 
     load2 = pltpu.make_async_copy(pot.at[1], p2, local_sem.at[0])
     load1 = pltpu.make_async_copy(pot.at[0], p1, local_sem.at[1])
@@ -163,7 +171,6 @@
 
     lane = iota((rows, LANES), 1)
     lane_group = lane // 8
-    lane_t = iota((tall, LANES), 1)
 
     def split(source, put):
         def body(i, carry):
@@ -181,8 +188,8 @@
         v1[b, EDGE : EDGE + rows, :] = value
 
     def sides(s):
-        before = tiles[lax.rem(s + (blocks - 1), blocks)]
-        after = tiles[lax.rem(s + 1, blocks)]
+        before = tiles[(s + (blocks - 1)) & (blocks - 1)]
+        after = tiles[(s + 1) & (blocks - 1)]
         return jnp.where(lane >= LANES // 2, before, after)
 
     def pack(i):
@@ -274,38 +281,65 @@
     def second(x, s1, s2, s3, s4):
         return 16.0 * (s1 - s3) + 64.0 * s2 + s4 - 130.0 * x
 
+    sub = iota((8, LANES), 0)
+    lane8 = iota((8, LANES), 1)
+    eight = rows // 2
+
+    def thirds(ref, f):
+        even = ref[f, pl.ds(EDGE, eight, stride=2), :]
+        odd = ref[f, pl.ds(EDGE + 1, eight, stride=2), :]
+        return even, odd, jnp.where(sub < EDGE, ref[f, 0:8, :], ref[f, tall - 8 : tall, :])
+
     def derive(ref, f, t, j):
-        x = ref[f]
-        ahead = [pltpu.roll(jnp.where(lane_t < k, t, x), LANES - k, 1) for k in range(1, 5)]
-        behind = [pltpu.roll(jnp.where(lane_t >= LANES - k, t, x), k, 1) for k in range(1, 5)]
-        c1s[j] = 8.0 * (ahead[0] - behind[0]) - (ahead[1] - behind[1])
-        ccs[j] = second(x, *[a + b for a, b in zip(ahead, behind)])
-
-        def tap(k):
-            return ref[f, EDGE + k : EDGE + k + rows, :]
-
-        def tap_c(k):
-            return c1s[j, EDGE + k : EDGE + k + rows, :]
-
-        up = [tap(k) for k in range(1, 5)]
-        low = [tap(-k) for k in range(1, 5)]
-        slope_r = 8.0 * (up[0] - low[0]) - (up[1] - low[1])
-        curve_rr = second(tap(0), *[a + b for a, b in zip(up, low)])
-        curve_rc = 8.0 * (tap_c(1) - tap_c(-1)) - (tap_c(2) - tap_c(-2))
-        curve_cc = ccs[j, EDGE : EDGE + rows, :]
-        return slope_r, tap_c(0), curve_rr, curve_rc, curve_cc
+        x = thirds(ref, f)
+
+        def ahead(p, k):
+            return pltpu.roll(jnp.where(lane8 < k, t[p], x[p]), LANES - k, 1)
+
+        def behind(p, k):
+            return pltpu.roll(jnp.where(lane8 >= LANES - k, t[p], x[p]), k, 1)
+
+        slope_c, curve_cc = [], []
+        for p in range(3):
+            a1, b1, a2, b2 = ahead(p, 1), behind(p, 1), ahead(p, 2), behind(p, 2)
+            slope_c.append(8.0 * (a1 - b1) - (a2 - b2))
+            if p < 2:
+                curve_cc.append(second(x[p], a1 + b1, a2 + b2, ahead(p, 3) + behind(p, 3), ahead(p, 4) + behind(p, 4)))
+        for p in range(2):
+            c1s[j, pl.ds(EDGE + p, eight, stride=2), :] = slope_c[p]
+        c1s[j, 0:EDGE, :] = slope_c[2][:EDGE]
+        c1s[j, tall - EDGE : tall, :] = slope_c[2][EDGE:]
+        c = {EDGE: slope_c[0], EDGE + 1: slope_c[1]}
+        r = {EDGE: x[0], EDGE + 1: x[1]}
+        for at in (2, 3, 6, 7):
+            c[at] = c1s[j, pl.ds(at, eight, stride=2), :]
+        for at in (0, 1, 2, 3, 6, 7, 8, 9):
+            r[at] = ref[f, pl.ds(at, eight, stride=2), :]
+        slope_r, curve_rr, curve_rc = [], [], []
+        for p in range(2):
+            m = EDGE + p
+            slope_r.append(8.0 * (r[m + 1] - r[m - 1]) - (r[m + 2] - r[m - 2]))
+            curve_rr.append(second(r[m], *[r[m + k] + r[m - k] for k in range(1, 5)]))
+            curve_rc.append(8.0 * (c[m + 1] - c[m - 1]) - (c[m + 2] - c[m - 2]))
+        return slope_r, slope_c, curve_rr, curve_rc, curve_cc
 
     def near_group(g):
         for j in range(GROUP):
             b = g * GROUP + j
-            before = v1[lax.rem(b + (blocks - 1), blocks)]
-            after = v1[lax.rem(b + 1, blocks)]
-            slope_r, slope_c, curve_rr, curve_rc, curve_cc = derive(v1, b, jnp.where(lane_t >= LANES // 2, before, after), j)
-            near[b, 0 * rows : 1 * rows, :] = two * (curve_rr + curve_cc)
-            near[b, 1 * rows : 2 * rows, :] = two * (curve_cc - curve_rr)
-            near[b, 2 * rows : 3 * rows, :] = (2.0 * two) * curve_rc
-            near[b, 3 * rows : 4 * rows, :] = (one * beta_one) * slope_r
-            near[b, 4 * rows : 5 * rows, :] = (one * beta_one) * slope_c
+            before = thirds(v1, b - 1 if j > 0 else lax.rem(b + (blocks - 1), blocks))
+            after = thirds(v1, b + 1 if j < GROUP - 1 else lax.rem(b + 1, blocks))
+            t = [jnp.where(lane8 >= LANES // 2, before[p], after[p]) for p in range(3)]
+            slope_r, slope_c, curve_rr, curve_rc, curve_cc = derive(v1, b, t, j)
+            for p in range(2):
+                values = (
+                    two * (curve_rr[p] + curve_cc[p]),
+                    two * (curve_cc[p] - curve_rr[p]),
+                    (2.0 * two) * curve_rc[p],
+                    (one * beta_one) * slope_r[p],
+                    (one * beta_one) * slope_c[p],
+                )
+                for k, value in enumerate(values):
+                    near[b, k * rows + p * eight : k * rows + (p + 1) * eight, :] = value
 
     def near_groups(begin, end):
         def body(g, carry):
@@ -324,16 +358,16 @@
                 for k in kinds:
                     if k == 0:
                         s = tab[5, f]
-                        v, c = tiles[s], pltpu.roll(sides(s), (8 * j + 4) % LANES, 1)
+                        v, c = tiles[s], sides(s)
                     else:
                         ref = stores[k - 1]
-                        limit = ref.shape[0] - 1
-                        v = ref[jnp.minimum(tab[2, f], limit)]
-                        c = ref[jnp.minimum(tab[3, f], limit)]
-                        c = pltpu.roll(c, tab[4, f], 1)
+                        at_v, at_c = tab[2, f], tab[3, f]
+                        if any(k2 > 0 and stores[k2 - 1].shape[0] > ref.shape[0] for k2 in kinds):
+                            at_v, at_c = jnp.minimum(at_v, ref.shape[0] - 1), jnp.minimum(at_c, ref.shape[0] - 1)
+                        v, c = ref[at_v], ref[at_c]
                     value = v if value is None else jnp.where(kind == k, v, value)
                     cols = c if cols is None else jnp.where(kind == k, c, cols)
-                halo = jnp.where(lane_group == j, cols, halo)
+                halo = jnp.where(lane_group == j, pltpu.roll(cols, tab[4, f], 1), halo)
                 v2[g * PACKET + j, EDGE : EDGE + rows, :] = value
             v2[g * PACKET + GROUP, EDGE : EDGE + rows, :] = halo
             return carry
@@ -347,25 +381,32 @@
 
     def combine(begin, end):
         def body(g, carry):
-            halo = v2[g * PACKET + GROUP]
+            halo = thirds(v2, g * PACKET + GROUP)
             for j in range(GROUP):
                 f = g * GROUP + j
-                t = pltpu.roll(halo, (LANES - 8 * j - 4) % LANES, 1)
+                t = [pltpu.roll(h, (LANES - 8 * j - 4) % LANES, 1) for h in halo]
                 far_r, far_c, far_rr, far_rc, far_cc = derive(v2, g * PACKET + j, t, j)
                 n = near[tab[7, f]]
-                n_sum, n_diff, n_rc2, n_r, n_c = (n[k * rows : (k + 1) * rows] for k in range(5))
-                s = scale * (far_rr + far_cc)
-                d = scale * (far_cc - far_rr)
-                r = scale * far_rc
-                d_half = half_far * d
-                r_far = near_far * r
-                rest = half_one - half_far * s
-                out[f, 0 * rows : 1 * rows, :] = s + n_sum * rest - d_half * n_diff - r_far * n_rc2
-                out[f, 1 * rows : 2 * rows, :] = d + n_diff * rest - d_half * n_sum
-                out[f, 2 * rows : 3 * rows, :] = (r + r) + n_rc2 * rest - r_far * n_sum
-                out[f, 3 * rows : 4 * rows, :] = r_far * n_diff - n_rc2 * d_half
-                out[f, 4 * rows : 5 * rows, :] = n_r + slope_scale * far_r
-                out[f, 5 * rows : 6 * rows, :] = n_c + slope_scale * far_c
+                for p in range(2):
+                    n_sum, n_diff, n_rc2, n_r, n_c = (
+                        n[k * rows + p * eight : k * rows + (p + 1) * eight] for k in range(5)
+                    )
+                    s = scale * (far_rr[p] + far_cc[p])
+                    d = scale * (far_cc[p] - far_rr[p])
+                    r = scale * far_rc[p]
+                    d_half = half_far * d
+                    r_far = near_far * r
+                    rest = half_one - half_far * s
+                    results = (
+                        s + n_sum * rest - d_half * n_diff - r_far * n_rc2,
+                        d + n_diff * rest - d_half * n_sum,
+                        (r + r) + n_rc2 * rest - r_far * n_sum,
+                        r_far * n_diff - n_rc2 * d_half,
+                        n_r + slope_scale * far_r[p],
+                        n_c + slope_scale * far_c[p],
+                    )
+                    for k, value in enumerate(results):
+                        out[f, pl.ds(k * rows + p, eight, stride=2), :] = value
             return carry
 
         lax.fori_loop(begin, end, body, 0)
@@ -381,28 +422,17 @@
                 arrival(way, hop, c).wait_recv()
 
     groups = blocks // GROUP
-    relays = [(hop, c) for hop in range(1, HALF) for c in range(hops[hop])]
-    late = [(hop, c) for hop, c in relays if hop == HALF - 1]
-    early = [pair for pair in relays if pair not in late]
-    share = max(1, -(-groups // (len(early) - 1)))
-    done = 0
-    for i, (hop, c) in enumerate(early):
-        forward(hop, c)
-        if i == 0:
-            for copy in edges1:
-                copy.wait_recv()
-        upto = min(groups, done + share)
-        if upto > done:
-            near_groups(done, upto)
-        done = upto
-    if done < groups:
-        near_groups(done, groups)
-
-    bounds = [0] + list(ends)
-    moved = [edges(v2, bounds[p] * PACKET, bounds[p + 1] * PACKET, 1 + p) for p in range(len(ends))]
-
-    def begin_phase(p, kinds):
-        gather(bounds[p], bounds[p + 1], kinds)
+    bounds = [0] + [end for end, _, _ in phases]
+    moved = [edges(v2, bounds[p] * PACKET, bounds[p + 1] * PACKET, 1 + p) for p in range(len(phases))]
+    landed = set()
+
+    def begin_phase(p):
+        _, least, reach = phases[p]
+        for hop in range(reach):
+            if hop not in landed:
+                land(hop)
+                landed.add(hop)
+        gather(bounds[p], bounds[p + 1], range(least, reach + 1))
         for copy in moved[p]:
             copy.start()
 
@@ -411,26 +441,43 @@
             copy.wait_recv()
         combine(bounds[p], bounds[p + 1])
 
-    land(0)
-    land(1)
-    if single:
-        for hop, c in late:
+    if len(phases) < 3:
+        for hop in range(1, HALF):
+            for c in range(hops[hop]):
+                forward(hop, c)
+        for copy in edges1:
+            copy.wait_recv()
+        near_groups(0, groups)
+        for p in range(len(phases)):
+            begin_phase(p)
+            end_phase(p)
+    else:
+        early = [(hop, c) for hop in (1, 2) for c in range(hops[hop])]
+        share = -(-groups // (len(early) - 1))
+        done = began = 0
+        for i, (hop, c) in enumerate(early):
             forward(hop, c)
-        land(2)
-        land(3)
-        begin_phase(0, (0, 1, 2, 3))
-        end_phase(0)
-    else:
-        begin_phase(0, (0, 1))
-        for hop, c in late:
-            forward(hop, c)
-        end_phase(0)
-        land(2)
-        begin_phase(1, (1, 2))
-        land(3)
-        begin_phase(2, (1, 2, 3))
-        end_phase(1)
-        end_phase(2)
+            if i == 0:
+                for copy in edges1:
+                    copy.wait_recv()
+            upto = min(groups, done + share)
+            if upto > done:
+                near_groups(done, upto)
+            done = upto
+            if phases[0][2] == 1 and i == hops[1] - 1:
+                begin_phase(0)
+                began = 1
+        if began:
+            end_phase(0)
+        begin_phase(began)
+        for c in range(hops[3]):
+            forward(3, c)
+        end_phase(began)
+        for p in range(began + 1, len(phases)):
+            begin_phase(p)
+            if p > began + 1:
+                end_phase(p - 1)
+        end_phase(len(phases) - 1)
 
     for copy in edges1:
         copy.wait_send()
@@ -445,7 +492,7 @@
 
 def exchange(index, tab, ratios, potentials):
     plan = PLANS[index]
-    hops, ends = plan
+    hops, phases = plan
     rows, columns = potentials.shape[1:]
     blocks = columns // LANES
     _, number = chunk_base(hops)
@@ -468,12 +515,11 @@
             pltpu.VMEM((packets, tall, LANES), f32),
             pltpu.VMEM((blocks, 5 * rows, LANES), f32),
             pltpu.VMEM((GROUP, tall, LANES), f32),
-            pltpu.VMEM((GROUP, tall, LANES), f32),
             pltpu.SemaphoreType.DMA((2,)),
             pltpu.SemaphoreType.DMA((2 * number,)),
             pltpu.SemaphoreType.DMA((2 * number,)),
-            pltpu.SemaphoreType.DMA((2 + 2 * len(ends),)),
-            pltpu.SemaphoreType.DMA((2 + 2 * len(ends),)),
+            pltpu.SemaphoreType.DMA((2 + 2 * len(phases),)),
+            pltpu.SemaphoreType.DMA((2 + 2 * len(phases),)),
         ],
         compiler_params=pltpu.CompilerParams(
             collective_id=index, has_side_effects=True, vmem_limit_bytes=30 * 2**20
@@ -484,9 +530,9 @@
 
 def arrange_kernel(tab, fields, conv, shear, rot, disp):
     g = pl.program_id(0)
-    rows = conv.shape[0]
-    for j in range(GROUP):
-        value = fields[tab[8, g * GROUP + j]]
+    rows, wide = conv.shape
+    for j in range(wide // LANES):
+        value = fields[tab[8, g * (wide // LANES) + j]]
         part = [value[k * rows : (k + 1) * rows] for k in range(6)]
         spot = slice(j * LANES, (j + 1) * LANES)
         conv[:, spot] = part[0]
@@ -499,7 +545,7 @@
 
 def arrange(tab, fields, rows):
     columns = fields.shape[0] * LANES
-    wide = GROUP * LANES
+    wide = columns // 4
     f32 = jnp.float32
     flat = jax.ShapeDtypeStruct((rows, columns), f32)
     pair = jax.ShapeDtypeStruct((2, rows, columns), f32)
@@ -524,14 +570,13 @@
         out_shape=jax.ShapeDtypeStruct((16, blocks), jnp.int32),
         in_specs=[vmem, vmem],
         out_specs=vmem,
-        compiler_params=pltpu.CompilerParams(vmem_limit_bytes=4 * 2**20),
         name="table",
     )(row_offset.reshape(1, blocks), col_offset.reshape(1, blocks))
     def run(index, tab, ratios, potentials):
         return arrange(tab, exchange(index, tab, ratios, potentials), potentials.shape[1])
 
-    return lax.cond(
-        tab[9, 0] == 0, functools.partial(run, 0), functools.partial(run, 1), tab, ratios, potentials
+    return lax.switch(
+        tab[9, 0], [functools.partial(run, i) for i in range(len(PLANS))], tab, ratios, potentials
     )
 
 

time: 74.6 us -> 68.7 us (0.921); the launches traced: 74.4 us -> 67.5 us
  Pallas kernels: 71.1 us -> 65.7 us
  local copies, waits for them, and re-layouts: 1.82 us -> 0.51 us
    pallas_call x1, Pallas kernels: 65.9 us -> 60.7 us  [exchange(): pl.pallas_call(functools.partial(exchange_kernel, plan), out_shape=jax.Sh...]
    unnamed x4 -> x0, local copies, waits for them, and re-layouts: 1.3 us -> none
    pallas_call x1, Pallas kernels: 4.81 us -> 3.88 us  [arrange(): pl.pallas_call(arrange_kernel, grid=(columns // wide,), out_shape=(flat,...]
where the time goes in v3:
time: 68.7 us; the launch traced here: 67.5 us
  Pallas kernels  65.7 us (96%)
  between operations  1.29 us (2%)
    pallas_call x1, Pallas kernels, exchange(): pl.pallas_call(functools.partial(exchange_kernel, plan), out_shape=jax.Sh...  60.7 us
    pallas_call x1, Pallas kernels, arrange(): pl.pallas_call(arrange_kernel, grid=(columns // wide,), out_shape=(flat,...  3.88 us

profile of v3, /device:TPU:528, one launch (start us, length us, event | category | flops | bytes accessed | tf_op | source)
XLA Modules:
  0.0 67.5 jit_solution(5299486470386293861)
XLA Ops:
  0.6 1.1 %table.1 = s32[16,128]{1,0:T(8,128)S(1)} custom-call(s32[1,128]{1,0:T(1,128)} %bitcast.3, s32[1,128]{1,0:T(1,128)} %bitcast.4), custom_call_target="tpu_custom_call" | custom-call | tf_op jit(solution)/shard_map/table/pallas_call | solution.py:568
  1.7 0.5 slice.4
  2.9 64.6 %conditional.1 = ((f32[16,16384]{1,0:T(8,128)}, f32[2,16,16384]{2,1,0:T(8,128)}, f32[16,16384]{1,0:T(8,128)}, f32[2,16,16384]{2,1,0:T(8,128)})) conditional(s32[]{:T(128)} %bitcast.2, (s32[16,128]{1,0:T(8,128)S(1)}, f32[3]{0:T(128)}, f32[2,16,16384]{2,1,0:T(8,128)}) %tuple.16, (s32[16,128]{1,0:T(8,128)S(1)}, f32[3]{0:T(128)}, ...), branch_computations={%region_0.0_spmd, %region_1.0_spmd, %region_2.0_spmd} | conditional | bytes 8 | solution.py:578
  2.9 60.7 %exchange0.1.fields = f32[128,96,128]{2,1,0:T(8,128)S(1)} custom-call(s32[16,128]{1,0:T(8,128)S(1)} %get-tuple-element.18.tab, f32[3]{0:T(128)} %get-tuple-element.53.ratios, f32[2,16,16384]{2,1,0:T(8,128)} %get-tuple-element.56.pot), custom_call_target="tpu_custom_call" | custom-call | tf_op jit(solution)/shard_map/cond/branch_0_fun/exchange0/pallas_call | solution.py:503
  63.6 3.9 %arrange.3 = (f32[16,16384]{1,0:T(8,128)}, f32[2,16,16384]{2,1,0:T(8,128)}, f32[16,16384]{1,0:T(8,128)}, f32[2,16,16384]{2,1,0:T(8,128)}) custom-call(s32[16,128]{1,0:T(8,128)S(1)} %get-tuple-element.18.tab, f32[128,96,128]{2,1,0:T(8,128)S(1)} %exchange0.1.fields), custom_call_target="tpu_custom_call" | custom-call | tf_op jit(solution)/shard_map/cond/branch_0_fun/arrange/pallas_call | solution.py:554

commit v4 on v3

--- a/solution.py
+++ b/solution.py
@@ -17,7 +17,7 @@
 
 PLANS = (
     ((4, 3, 2, 1), ((2, 0, 1), (4, 1, 2), (6, 2, 3), (8, 3, 4))),
-    ((4, 3, 2, 1), ((3, 0, 2), (6, 1, 3), (8, 2, 4))),
+    ((5, 4, 3, 2), ((3, 0, 2), (6, 1, 3), (8, 2, 4))),
     ((8, 8, 8, 4), ((8, 0, 4),)),
 )
 STORES = ((0,), (1,), (2,), (3,))
@@ -78,6 +78,17 @@
     load_a = total(jnp.where(row < HALF, row, 0.0))
     load_b = total(jnp.where(row > HALF, RB - row, 0.0))
     take_a = jnp.clip(jnp.floor((load_b + HALF * n_half - load_a) / (2 * HALF) + 0.5), 0.0, n_half)
+
+    def room(side):
+        most = n_half
+        for hop, count in enumerate(PLANS[0][0]):
+            most = jnp.minimum(most, count * GROUP - total((side & (dist > hop)).astype(f32)))
+        return most
+
+    room_a, room_b = room((row > 0) & (row < HALF)), room(row > HALF)
+    held = jnp.minimum(jnp.maximum(take_a, n_half - room_b), room_a)
+    possible = (room_a >= 0) & (room_b >= 0) & (room_a + room_b >= n_half)
+    take_a = jnp.where(possible, held, take_a)
     rank_half = down(jnp.where(sub2 < lane2, column(halfway), 0.0))
     way = jnp.where(row == 0, 0.0, jnp.where(row < HALF, 1.0, 2.0))
     way = jnp.where((row == HALF) & (rank_half < take_a), 1.0, way)

time: 68.7 us -> 68.7 us (level)
  no operation moved by 1% of the time
where the time goes in v4:
time: 68.7 us; the launch traced here: 67.5 us
  Pallas kernels  65.7 us (96%)
  between operations  1.29 us (2%)
    pallas_call x1, Pallas kernels, exchange(): pl.pallas_call(functools.partial(exchange_kernel, plan), out_shape=jax.Sh...  60.7 us
    pallas_call x1, Pallas kernels, arrange(): pl.pallas_call(arrange_kernel, grid=(columns // wide,), out_shape=(flat,...  3.88 us

profile of v4, /device:TPU:528, one launch (start us, length us, event | category | flops | bytes accessed | tf_op | source)
XLA Modules:
  0.0 67.5 jit_solution(12137444496594839315)
XLA Ops:
  0.6 1.1 %table.1 = s32[16,128]{1,0:T(8,128)S(1)} custom-call(s32[1,128]{1,0:T(1,128)} %bitcast.3, s32[1,128]{1,0:T(1,128)} %bitcast.4), custom_call_target="tpu_custom_call" | custom-call | tf_op jit(solution)/shard_map/table/pallas_call | solution.py:579
  1.7 0.5 slice.4
  2.9 64.6 %conditional.1 = ((f32[16,16384]{1,0:T(8,128)}, f32[2,16,16384]{2,1,0:T(8,128)}, f32[16,16384]{1,0:T(8,128)}, f32[2,16,16384]{2,1,0:T(8,128)})) conditional(s32[]{:T(128)} %bitcast.2, (s32[16,128]{1,0:T(8,128)S(1)}, f32[3]{0:T(128)}, f32[2,16,16384]{2,1,0:T(8,128)}) %tuple.16, (s32[16,128]{1,0:T(8,128)S(1)}, f32[3]{0:T(128)}, ...), branch_computations={%region_0.0_spmd, %region_1.0_spmd, %region_2.0_spmd} | conditional | bytes 8 | solution.py:589
  2.9 60.7 %exchange0.1.fields = f32[128,96,128]{2,1,0:T(8,128)S(1)} custom-call(s32[16,128]{1,0:T(8,128)S(1)} %get-tuple-element.18.tab, f32[3]{0:T(128)} %get-tuple-element.53.ratios, f32[2,16,16384]{2,1,0:T(8,128)} %get-tuple-element.56.pot), custom_call_target="tpu_custom_call" | custom-call | tf_op jit(solution)/shard_map/cond/branch_0_fun/exchange0/pallas_call | solution.py:514
  63.6 3.9 %arrange.3 = (f32[16,16384]{1,0:T(8,128)}, f32[2,16,16384]{2,1,0:T(8,128)}, f32[16,16384]{1,0:T(8,128)}, f32[2,16,16384]{2,1,0:T(8,128)}) custom-call(s32[16,128]{1,0:T(8,128)S(1)} %get-tuple-element.18.tab, f32[128,96,128]{2,1,0:T(8,128)S(1)} %exchange0.1.fields), custom_call_target="tpu_custom_call" | custom-call | tf_op jit(solution)/shard_map/cond/branch_0_fun/arrange/pallas_call | solution.py:565

commit v5 on v4

--- a/solution.py
+++ b/solution.py
@@ -159,7 +159,7 @@
     tab_ref[...] = jnp.concatenate(rows, axis=0).astype(jnp.int32)
 
 
-def exchange_kernel(plan, tab, ratios, pot, out, p1, p2, tiles, sent, got_a, got_b, got_c, got_d, v1, v2, near, c1s,
+def exchange_kernel(plan, tab, ratios, pot, out, p1, p2, tiles, sent, got_a, got_b, got_c, got_d, v1, v2, near, c1s, turned,
                     local_sem, send_sem, recv_sem, edge_send, edge_recv):
     hops, phases = plan
     base, number = chunk_base(hops)
@@ -394,8 +394,11 @@
         def body(g, carry):
             halo = thirds(v2, g * PACKET + GROUP)
             for j in range(GROUP):
+                for p in range(3):
+                    turned[j, 8 * p : 8 * p + 8, :] = pltpu.roll(halo[p], (LANES - 8 * j - 4) % LANES, 1)
+            for j in range(GROUP):
                 f = g * GROUP + j
-                t = [pltpu.roll(h, (LANES - 8 * j - 4) % LANES, 1) for h in halo]
+                t = [turned[j, 8 * p : 8 * p + 8, :] for p in range(3)]
                 far_r, far_c, far_rr, far_rc, far_cc = derive(v2, g * PACKET + j, t, j)
                 n = near[tab[7, f]]
                 for p in range(2):
@@ -526,6 +529,7 @@
             pltpu.VMEM((packets, tall, LANES), f32),
             pltpu.VMEM((blocks, 5 * rows, LANES), f32),
             pltpu.VMEM((GROUP, tall, LANES), f32),
+            pltpu.VMEM((GROUP, tall, LANES), f32),
             pltpu.SemaphoreType.DMA((2,)),
             pltpu.SemaphoreType.DMA((2 * number,)),
             pltpu.SemaphoreType.DMA((2 * number,)),

time: 68.7 us -> 64.9 us (0.945)
  Pallas kernels: 65.7 us -> 62.1 us
    pallas_call x1, Pallas kernels: 60.7 us -> 57.1 us  [exchange(): pl.pallas_call(functools.partial(exchange_kernel, plan), out_shape=jax.Sh...]
where the time goes in v5:
time: 64.9 us; the launch traced here: 63.9 us
  Pallas kernels  62.1 us (96%)
  between operations  1.29 us (2%)
    pallas_call x1, Pallas kernels, exchange(): pl.pallas_call(functools.partial(exchange_kernel, plan), out_shape=jax.Sh...  57.1 us
    pallas_call x1, Pallas kernels, arrange(): pl.pallas_call(arrange_kernel, grid=(columns // wide,), out_shape=(flat,...  3.88 us

profile of v5, /device:TPU:528, one launch (start us, length us, event | category | flops | bytes accessed | tf_op | source)
XLA Modules:
  0.0 63.9 jit_solution(10993388218959900825)
XLA Ops:
  0.6 1.1 %table.1 = s32[16,128]{1,0:T(8,128)S(1)} custom-call(s32[1,128]{1,0:T(1,128)} %bitcast.3, s32[1,128]{1,0:T(1,128)} %bitcast.4), custom_call_target="tpu_custom_call" | custom-call | tf_op jit(solution)/shard_map/table/pallas_call | solution.py:583
  1.7 0.5 slice.4
  2.9 61.0 %conditional.1 = ((f32[16,16384]{1,0:T(8,128)}, f32[2,16,16384]{2,1,0:T(8,128)}, f32[16,16384]{1,0:T(8,128)}, f32[2,16,16384]{2,1,0:T(8,128)})) conditional(s32[]{:T(128)} %bitcast.2, (s32[16,128]{1,0:T(8,128)S(1)}, f32[3]{0:T(128)}, f32[2,16,16384]{2,1,0:T(8,128)}) %tuple.16, (s32[16,128]{1,0:T(8,128)S(1)}, f32[3]{0:T(128)}, ...), branch_computations={%region_0.0_spmd, %region_1.0_spmd, %region_2.0_spmd} | conditional | bytes 8 | solution.py:593
  2.9 57.1 %exchange0.1.fields = f32[128,96,128]{2,1,0:T(8,128)S(1)} custom-call(s32[16,128]{1,0:T(8,128)S(1)} %get-tuple-element.18.tab, f32[3]{0:T(128)} %get-tuple-element.53.ratios, f32[2,16,16384]{2,1,0:T(8,128)} %get-tuple-element.56.pot), custom_call_target="tpu_custom_call" | custom-call | tf_op jit(solution)/shard_map/cond/branch_0_fun/exchange0/pallas_call | solution.py:517
  60.0 3.9 %arrange.3 = (f32[16,16384]{1,0:T(8,128)}, f32[2,16,16384]{2,1,0:T(8,128)}, f32[16,16384]{1,0:T(8,128)}, f32[2,16,16384]{2,1,0:T(8,128)}) custom-call(s32[16,128]{1,0:T(8,128)S(1)} %get-tuple-element.18.tab, f32[128,96,128]{2,1,0:T(8,128)S(1)} %exchange0.1.fields), custom_call_target="tpu_custom_call" | custom-call | tf_op jit(solution)/shard_map/cond/branch_0_fun/arrange/pallas_call | solution.py:569

commit v6 on v5

--- a/solution.py
+++ b/solution.py
@@ -560,7 +560,7 @@
 
 def arrange(tab, fields, rows):
     columns = fields.shape[0] * LANES
-    wide = columns // 4
+    wide = columns // 2
     f32 = jnp.float32
     flat = jax.ShapeDtypeStruct((rows, columns), f32)
     pair = jax.ShapeDtypeStruct((2, rows, columns), f32)

time: 64.9 us -> 64.7 us (level)
  no operation moved by 1% of the time
where the time goes in v6:
time: 64.7 us; the launch traced here: 63.8 us
  Pallas kernels  62 us (96%)
  between operations  1.29 us (2%)
    pallas_call x1, Pallas kernels, exchange(): pl.pallas_call(functools.partial(exchange_kernel, plan), out_shape=jax.Sh...  57.1 us
    pallas_call x1, Pallas kernels, arrange(): pl.pallas_call(arrange_kernel, grid=(columns // wide,), out_shape=(flat,...  3.75 us

profile of v6, /device:TPU:528, one launch (start us, length us, event | category | flops | bytes accessed | tf_op | source)
XLA Modules:
  0.0 63.8 jit_solution(7668508827257940693)
XLA Ops:
  0.6 1.1 %table.1 = s32[16,128]{1,0:T(8,128)S(1)} custom-call(s32[1,128]{1,0:T(1,128)} %bitcast.3, s32[1,128]{1,0:T(1,128)} %bitcast.4), custom_call_target="tpu_custom_call" | custom-call | tf_op jit(solution)/shard_map/table/pallas_call | solution.py:583
  1.7 0.5 slice.4
  2.9 60.9 %conditional.1 = ((f32[16,16384]{1,0:T(8,128)}, f32[2,16,16384]{2,1,0:T(8,128)}, f32[16,16384]{1,0:T(8,128)}, f32[2,16,16384]{2,1,0:T(8,128)})) conditional(s32[]{:T(128)} %bitcast.2, (s32[16,128]{1,0:T(8,128)S(1)}, f32[3]{0:T(128)}, f32[2,16,16384]{2,1,0:T(8,128)}) %tuple.16, (s32[16,128]{1,0:T(8,128)S(1)}, f32[3]{0:T(128)}, ...), branch_computations={%region_0.0_spmd, %region_1.0_spmd, %region_2.0_spmd} | conditional | bytes 8 | solution.py:593
  2.9 57.1 %exchange0.1.fields = f32[128,96,128]{2,1,0:T(8,128)S(1)} custom-call(s32[16,128]{1,0:T(8,128)S(1)} %get-tuple-element.18.tab, f32[3]{0:T(128)} %get-tuple-element.53.ratios, f32[2,16,16384]{2,1,0:T(8,128)} %get-tuple-element.56.pot), custom_call_target="tpu_custom_call" | custom-call | tf_op jit(solution)/shard_map/cond/branch_0_fun/exchange0/pallas_call | solution.py:517
  60.0 3.8 %arrange.3 = (f32[16,16384]{1,0:T(8,128)}, f32[2,16,16384]{2,1,0:T(8,128)}, f32[16,16384]{1,0:T(8,128)}, f32[2,16,16384]{2,1,0:T(8,128)}) custom-call(s32[16,128]{1,0:T(8,128)S(1)} %get-tuple-element.18.tab, f32[128,96,128]{2,1,0:T(8,128)S(1)} %exchange0.1.fields), custom_call_target="tpu_custom_call" | custom-call | tf_op jit(solution)/shard_map/cond/branch_0_fun/arrange/pallas_call | solution.py:569
